TPU v7x, 32 devices: a whole 2x2x4 slice. The times are simulated.
32 devices in a mesh: dp: 8 (over z, y), mp: 4 (over x, core).
Axes of the slice: x: 2, y: 2, z: 4, core: 2. Of those that a mesh axis runs over, the one named last changes fastest.
Arguments:
- queries: bfloat16 [128, 8192], P('dp', 'mp'), may hold values from -8 to 8
- incoming_key: bfloat16 [128, 1024], P('dp', 'mp'), may hold values from -4 to 4
- incoming_value: bfloat16 [128, 1024], P('dp', 'mp'), may hold values from -4 to 4
- key_cache: bfloat16 [256, 256, 1024], P('dp', None, 'mp'), may hold values from -8 to 8
- cached_values: bfloat16 [256, 256, 1024], P('dp', None, 'mp'), may hold values from -4 to 4
- task_key_scale: bfloat16 [256, 1024], P(None, 'mp'), may hold values from 0.099609375 to 1.8984375
- task_value_scale: bfloat16 [256, 1024], P(None, 'mp'), may hold values from 0.099609375 to 1.8984375
- out_weight: bfloat16 [8192, 8192], P('mp', 'dp'), may hold values from -0.0625 to 0.0625
- task_id: int32 [128], P('dp'), may hold values from 0 to 255, as said below
- cached_length: int32 [128], P('dp'), may hold values from 1 to 256, as said below
- task_owner: int32 [256], replicated, may hold values from 0 to 7, as said below
- cache_slot: int32 [128], P('dp'), may hold values from 0 to 31, as said below
Outputs:
- layer_out: bfloat16 [128, 8192], P('dp', 'mp')
Inputs may be any that keep to these rules, and one draw needn't show every extreme that they name: `task_owner`: every dp index owns the same number of tasks. `task_id`: among the 16 requests of one dp index at most 4 have tasks of one owner; in every draw one owner gets exactly 4 from every dp index. `cache_slot`: requests of one owner have distinct slots; one owner uses all 32. `cached_length`: every dp index has a request with 256 cached positions.
All inputs are finite; a program needn't handle non-finite values.
Results may differ from a plain program's by a relative error of at most 0.0073.
Values may be sent and summed in bfloat16 or wider, within the bound.
A program may use at most 128 MiB of HBM per device.

v0:
```python
import functools
import math

import jax
import jax.numpy as jnp
from jax import lax
from jax.experimental import pallas as pl
from jax.experimental.pallas import tpu as pltpu
from jax.sharding import PartitionSpec as P

KEY_VALUE_HEADS = 8
HEAD_SIZE = 128
QUERY_HEADS = 64
GROUP = QUERY_HEADS // KEY_VALUE_HEADS
META = 128
FIRST = 16
TOGETHER = 8
CHUNKS = 4
MESH = pl.DeviceIdType.MESH

masked_score = -1e30
f32 = jnp.float32
bf16 = jnp.bfloat16


def iota(shape, dim):
    return lax.broadcasted_iota(jnp.int32, shape, dim)


def to_column(row):
    n = row.shape[1]
    eye = iota((n, n), 0) == iota((n, n), 1)
    return jnp.sum(jnp.where(eye, row, 0.0), axis=1, keepdims=True)


def to_row(column):
    n = column.shape[0]
    eye = iota((n, n), 0) == iota((n, n), 1)
    return jnp.sum(jnp.where(eye, column, 0.0), axis=0, keepdims=True)


def factors(dp):
    inner = 2 ** (int(math.log2(dp)) // 2)
    return dp // inner, inner


def dot(a, b):
    return jnp.dot(a, b, preferred_element_type=f32)


def layer_kernel(
    dp,
    mp,
    query_ref,
    new_key_ref,
    new_value_ref,
    key_scale_ref,
    value_scale_ref,
    task_ref,
    length_ref,
    slot_ref,
    owner_ref,
    key_hbm,
    value_hbm,
    weight_hbm,
    out_ref,
    keys,
    values,
    weight,
    rows_f32,
    send_rows,
    recv_rows,
    slot_query,
    slot_small,
    slot_length,
    slot_context,
    context,
    selector,
    send_part,
    recv_part,
    local_sem,
    send_sem,
    recv_sem,
    along_send,
    along_recv,
    across_send,
    across_recv,
):
    me = lax.axis_index("dp")
    part = lax.axis_index("mp")
    rows, query_width = query_ref.shape
    kv_width = new_key_ref.shape[1]
    kv_heads = kv_width // HEAD_SIZE
    heads = kv_heads * GROUP
    task_total = key_scale_ref.shape[0]
    slots, positions, _ = keys.shape
    capacity = send_rows.shape[1]
    items = dp * capacity
    columns = weight.shape[1]
    blocks = dp // mp
    meta_at = query_width + 2 * kv_width
    chunks, chunk = context.shape[1:3]
    outer, inner = factors(dp)

    total = dp * mp
    here = me * mp + part
    barrier = pltpu.get_barrier_semaphore()

    def greet(k, carry):
        other = lax.rem(here + k, total)
        pl.semaphore_signal(
            barrier,
            inc=1,
            device_id=(other // mp, lax.rem(other, mp)),
            device_id_type=MESH,
        )
        return carry

    lax.fori_loop(1, total, greet, 0)

    fetches = [
        pltpu.make_async_copy(key_hbm, keys, local_sem.at[0]),
        pltpu.make_async_copy(value_hbm, values, local_sem.at[1]),
        pltpu.make_async_copy(weight_hbm, weight, local_sem.at[2]),
    ]
    for fetch in fetches:
        fetch.start()

    task_column = to_column(task_ref[...].astype(f32))
    length_column = to_column(length_ref[...].astype(f32))
    slot_column = to_column(slot_ref[...].astype(f32))
    picked = task_column == iota((rows, task_total), 1).astype(f32)
    owner_column = jnp.sum(
        jnp.where(picked, owner_ref[...].astype(f32), 0.0), axis=1, keepdims=True
    )
    owner_row = to_row(owner_column)
    earlier = iota((rows, rows), 1) < iota((rows, rows), 0)
    rank = jnp.sum(
        jnp.where(earlier & (owner_column == owner_row), 1.0, 0.0), axis=1, keepdims=True
    )
    position_row = to_row(owner_column * capacity + rank)
    packer = jnp.where(position_row == iota((items, rows), 0).astype(f32), 1.0, 0.0).astype(bf16)
    key_factor = dot(jnp.where(picked, 1.0, 0.0).astype(bf16), key_scale_ref[...])
    for h in range(heads):
        g = h // GROUP
        lanes = slice(h * HEAD_SIZE, (h + 1) * HEAD_SIZE)
        scaled = (
            query_ref[:, lanes].astype(f32) * key_factor[:, g * HEAD_SIZE : (g + 1) * HEAD_SIZE]
        ).astype(bf16)
        rows_f32[:, lanes] = dot(packer, scaled)
    rows_f32[:, query_width : query_width + kv_width] = dot(packer, new_key_ref[...])
    rows_f32[:, query_width + kv_width : meta_at] = dot(packer, new_value_ref[...])
    lane = iota((rows, META), 1)
    line = iota((rows, META), 0)
    task_high = jnp.floor(task_column * (1.0 / 128.0))
    task_low = task_column - task_high * 128.0
    facts = (
        jnp.where(lane == 0, slot_column + 1.0, 0.0)
        + jnp.where(lane == 1, length_column, 0.0)
        + jnp.where(lane == 2, task_high, 0.0)
        + jnp.where(lane == 3, task_low, 0.0)
    )
    shared = jnp.sum(
        jnp.where(lane == FIRST + line, owner_column, 0.0)
        + jnp.where(lane == FIRST + rows + line, slot_column, 0.0),
        axis=0,
        keepdims=True,
    )
    rows_f32[:, meta_at:] = dot(packer, facts.astype(bf16)) + shared
    for d in range(dp):
        send_rows[d] = rows_f32[d * capacity : (d + 1) * capacity, :].astype(bf16)

    pl.semaphore_wait(barrier, total - 1)

    def request_copy(k):
        return pltpu.make_async_remote_copy(
            src_ref=send_rows.at[lax.rem(me + k, dp)],
            dst_ref=recv_rows.at[me],
            send_sem=send_sem.at[0, k],
            recv_sem=recv_sem.at[0, k],
            device_id=(lax.rem(me + k, dp), part),
            device_id_type=MESH,
        )

    def request_arrival(k):
        return pltpu.make_async_remote_copy(
            src_ref=send_rows.at[0],
            dst_ref=recv_rows.at[lax.rem(me + dp - k, dp)],
            send_sem=send_sem.at[0, k],
            recv_sem=recv_sem.at[0, k],
            device_id=(lax.rem(me + k, dp), part),
            device_id_type=MESH,
        )

    for k in range(1, dp):
        request_copy(k).start()
    recv_rows[me] = send_rows[me]
    slot_query[...] = jnp.zeros_like(slot_query)
    for k in range(1, dp):
        request_arrival(k).wait_recv()

    for s in range(dp):
        rows_f32[s * capacity : (s + 1) * capacity, :] = recv_rows[s].astype(f32)
    facts_in = rows_f32[:, meta_at:]
    placing_row = to_row(facts_in[:, 0:1])
    placer = jnp.where(
        placing_row == iota((slots, items), 0).astype(f32) + 1.0, 1.0, 0.0
    ).astype(bf16)
    for h in range(heads):
        g = h // GROUP
        slot_query[:, h, g * HEAD_SIZE : (g + 1) * HEAD_SIZE] = dot(
            placer, rows_f32[:, h * HEAD_SIZE : (h + 1) * HEAD_SIZE].astype(bf16)
        )
    slot_small[0] = dot(placer, rows_f32[:, query_width : query_width + kv_width].astype(bf16))
    slot_small[1] = dot(placer, rows_f32[:, query_width + kv_width : meta_at].astype(bf16))
    slot_facts = dot(placer, facts_in.astype(bf16))
    slot_task = slot_facts[:, 2:3] * 128.0 + slot_facts[:, 3:4]
    slot_small[2] = dot(
        jnp.where(slot_task == iota((slots, task_total), 1).astype(f32), 1.0, 0.0).astype(bf16),
        value_scale_ref[...],
    )
    slot_length[...] = jnp.broadcast_to(slot_facts[:, 1:2], (slots, positions))

    fetches[0].wait()
    fetches[1].wait()
    inv_root = 1.0 / math.sqrt(HEAD_SIZE)
    key_line = iota((heads, positions), 1).astype(f32)

    def attend(n, carry):
        picks = [n * TOGETHER + i for i in range(TOGETHER)]
        scores, owns, weights, own_weights, sums, tops = [], [], [], [], [], []
        for s in picks:
            scores.append(
                lax.dot_general(
                    slot_query[s].astype(bf16),
                    keys[s],
                    (((1,), (1,)), ((), ())),
                    preferred_element_type=f32,
                )
                * inv_root
            )
        for s in picks:
            owns.append(
                jnp.sum(slot_query[s] * slot_small[0, pl.ds(s, 1), :], axis=1, keepdims=True)
                * inv_root
            )
        for i, s in enumerate(picks):
            visible = key_line < slot_length[pl.ds(s, 1), :]
            shown = jnp.where(visible, scores[i], masked_score)
            tops.append(jnp.maximum(jnp.max(shown, axis=1, keepdims=True), owns[i]))
        for i, s in enumerate(picks):
            visible = key_line < slot_length[pl.ds(s, 1), :]
            shown = jnp.where(visible, scores[i], masked_score)
            weights.append(jnp.where(visible, jnp.exp(shown - tops[i]), 0.0))
            own_weights.append(jnp.exp(owns[i] - tops[i]))
        blends = [dot(weights[i].astype(bf16), values[s]) for i, s in enumerate(picks)]
        for i in range(TOGETHER):
            sums.append(jnp.sum(weights[i], axis=1, keepdims=True) + own_weights[i])
        for i, s in enumerate(picks):
            one = pl.ds(s, 1)
            blended = blends[i] + own_weights[i].astype(bf16).astype(f32) * slot_small[1, one, :]
            attended = (blended / sums[i]).astype(bf16).astype(f32) * slot_small[2, one, :]
            for g in range(kv_heads):
                slot_context[s, g * GROUP : (g + 1) * GROUP, :] = attended[
                    g * GROUP : (g + 1) * GROUP, g * HEAD_SIZE : (g + 1) * HEAD_SIZE
                ]
        return carry

    column, line_in = me // inner, lax.rem(me, inner)

    def source_of(k):
        return lax.rem(column + outer - k, outer) * inner + line_in

    def along_copy(k, c, source):
        return pltpu.make_async_remote_copy(
            src_ref=context.at[source, c],
            dst_ref=context.at[source, c],
            send_sem=along_send.at[k, c],
            recv_sem=along_recv.at[k, c],
            device_id=(lax.rem(column + k, outer) * inner + line_in, part),
            device_id_type=MESH,
        )

    def across_copy(k, j, c, source):
        return pltpu.make_async_remote_copy(
            src_ref=context.at[source, c],
            dst_ref=context.at[source, c],
            send_sem=across_send.at[k, j, c],
            recv_sem=across_recv.at[k, j, c],
            device_id=(column * inner + lax.rem(line_in + j, inner), part),
            device_id_type=MESH,
        )

    def forward(c):
        for k in (outer - 1, *range(1, outer - 1)):
            along_copy(k, c, source_of(k)).wait_recv()
            for j in range(1, inner):
                across_copy(k, j, c, source_of(k)).start()

    for c in range(chunks):
        lax.fori_loop(c * chunk // TOGETHER, (c + 1) * chunk // TOGETHER, attend, 0)
        for h in range(heads):
            context[me, c, :, h * HEAD_SIZE : (h + 1) * HEAD_SIZE] = slot_context[
                c * chunk : (c + 1) * chunk, h, :
            ].astype(bf16)
        for k in range(1, outer):
            along_copy(k, c, me).start()
        for j in range(1, inner):
            across_copy(0, j, c, me).start()
        if c > 0:
            forward(c - 1)

    lane_r = iota((rows, META), 1)
    line_r = iota((rows, META), 0)
    for s in range(dp):
        fact_row = rows_f32[s * capacity : s * capacity + 1, meta_at:]
        owner_in = jnp.sum(
            jnp.where(lane_r == FIRST + line_r, fact_row, 0.0), axis=1, keepdims=True
        )
        slot_in = jnp.sum(
            jnp.where(lane_r == FIRST + rows + line_r, fact_row, 0.0), axis=1, keepdims=True
        )
        selector[s * rows : (s + 1) * rows, :] = jnp.where(
            owner_in * slots + slot_in == iota((rows, dp * slots), 1).astype(f32), 1.0, 0.0
        ).astype(bf16)
    fetches[2].wait()
    forward(chunks - 1)
    for c in range(chunks):
        for k in range(outer):
            for j in range(1, inner):
                source = lax.rem(column + outer - k, outer) * inner + lax.rem(
                    line_in + inner - j, inner
                )
                across_copy(k, j, c, source).wait_recv()

    arranged = dot(selector[...], context[...].reshape(dp * slots, query_width)).astype(bf16)
    send_part[...] = dot(arranged, weight[...]).astype(bf16).reshape(dp, rows, columns)

    target_part = me // blocks
    place = lax.rem(me, blocks) * mp + part

    def part_copy(k):
        target = lax.rem(me + k, dp)
        return pltpu.make_async_remote_copy(
            src_ref=send_part.at[target],
            dst_ref=recv_part.at[place],
            send_sem=send_sem.at[2, k],
            recv_sem=recv_sem.at[2, place],
            device_id=(target, target_part),
            device_id_type=MESH,
        )

    def part_arrival(j):
        return pltpu.make_async_remote_copy(
            src_ref=send_part.at[0],
            dst_ref=recv_part.at[j],
            send_sem=send_sem.at[2, 0],
            recv_sem=recv_sem.at[2, j],
            device_id=(me, part),
            device_id_type=MESH,
        )

    for k in range(1, dp):
        part_copy(k).start()

    @pl.when(target_part != part)
    def _():
        part_copy(0).start()

    @pl.when(target_part == part)
    def _():
        recv_part[place] = send_part[me]

    for j in range(dp):
        own_block = (part * blocks + j // mp == me) & (part == j % mp)

        @pl.when(jnp.logical_not(own_block))
        def _():
            part_arrival(j).wait_recv()

    for e in range(blocks):
        summed = recv_part[e * mp].astype(f32)
        for j in range(1, mp):
            summed = summed + recv_part[e * mp + j].astype(f32)
        out_ref[:, e * columns : (e + 1) * columns] = summed.astype(bf16)

    for k in range(1, dp):
        request_copy(k).wait_send()
        part_copy(k).wait_send()

    for c in range(chunks):
        for k in range(outer):
            if k > 0:
                along_copy(k, c, me).wait_send()
            for j in range(1, inner):
                across_copy(k, j, c, source_of(k)).wait_send()

    @pl.when(target_part != part)
    def _():
        part_copy(0).wait_send()


def on_device(
    dp,
    mp,
    queries,
    incoming_key,
    incoming_value,
    key_cache,
    cached_values,
    task_key_scale,
    task_value_scale,
    out_weight,
    task_id,
    cached_length,
    task_owner,
    cache_slot,
):
    rows, query_width = queries.shape
    kv_width = incoming_key.shape[1]
    slots = key_cache.shape[0]
    capacity = 2 * rows // dp
    items = dp * capacity
    columns = out_weight.shape[1]
    row_width = query_width + 2 * kv_width + META
    heads = query_width // HEAD_SIZE
    outer, inner = factors(dp)
    vmem = pl.BlockSpec(memory_space=pltpu.VMEM)
    away = pl.BlockSpec(memory_space=pl.ANY)
    return pl.pallas_call(
        functools.partial(layer_kernel, dp, mp),
        out_shape=jax.ShapeDtypeStruct((rows, dp * columns // mp), bf16),
        in_specs=[vmem] * 9 + [away] * 3,
        out_specs=vmem,
        scratch_shapes=[
            pltpu.VMEM(key_cache.shape, bf16),
            pltpu.VMEM(cached_values.shape, bf16),
            pltpu.VMEM(out_weight.shape, bf16),
            pltpu.VMEM((items, row_width), f32),
            pltpu.VMEM((dp, capacity, row_width), bf16),
            pltpu.VMEM((dp, capacity, row_width), bf16),
            pltpu.VMEM((slots, heads, kv_width), f32),
            pltpu.VMEM((3, slots, kv_width), f32),
            pltpu.VMEM((slots, key_cache.shape[1]), f32),
            pltpu.VMEM((slots, heads, HEAD_SIZE), f32),
            pltpu.VMEM((dp, CHUNKS, slots // CHUNKS, query_width), bf16),
            pltpu.VMEM((dp * rows, dp * slots), bf16),
            pltpu.VMEM((dp, rows, columns), bf16),
            pltpu.VMEM((dp, rows, columns), bf16),
            pltpu.SemaphoreType.DMA((3,)),
            pltpu.SemaphoreType.DMA((3, dp)),
            pltpu.SemaphoreType.DMA((3, dp)),
            pltpu.SemaphoreType.DMA((outer, CHUNKS)),
            pltpu.SemaphoreType.DMA((outer, CHUNKS)),
            pltpu.SemaphoreType.DMA((outer, inner, CHUNKS)),
            pltpu.SemaphoreType.DMA((outer, inner, CHUNKS)),
        ],
        compiler_params=pltpu.CompilerParams(
            collective_id=0, has_side_effects=True, vmem_limit_bytes=60 * 1024 * 1024
        ),
    )(
        queries,
        incoming_key,
        incoming_value,
        task_key_scale,
        task_value_scale,
        task_id.reshape(1, -1),
        cached_length.reshape(1, -1),
        cache_slot.reshape(1, -1),
        task_owner.reshape(1, -1),
        key_cache,
        cached_values,
        out_weight,
    )


def solution(mesh):
    placed = (
        P("dp", "mp"),
        P("dp", "mp"),
        P("dp", "mp"),
        P("dp", None, "mp"),
        P("dp", None, "mp"),
        P(None, "mp"),
        P(None, "mp"),
        P("mp", "dp"),
        P("dp"),
        P("dp"),
        P(),
        P("dp"),
    )
    return jax.shard_map(
        functools.partial(on_device, mesh.shape["dp"], mesh.shape["mp"]),
        mesh=mesh,
        in_specs=placed,
        out_specs=P("dp", "mp"),
        check_vma=False,
    )
```

profile of v0, /device:TPU:0, one launch (start us, length us, event | category | flops | bytes accessed | tf_op | source)
XLA Modules:
  0.0 39.4 jit_solution(15318382825774511149)
XLA Ops:
  0.0 38.0 %shard_map.118 = bf16[16,2048]{1,0:T(8,128)(2,1)} custom-call(bf16[16,2048]{1,0:T(8,128)(2,1)} %query_ref.1, bf16[16,256]{1,0:T(8,128)(2,1)} %new_key_ref.1, bf16[16,256]{1,0:T(8,128)(2,1)} %new_value_ref.1, bf16[256,256]{1,0:T(8,128)(2,1)} %key_scale_ref.1, bf16[256,256]{1,0:T(8,128)(2,1)} %value_scale_ref.1, s32[1,16]{1,0:T(1,128)} %bitcast.5, ...), custom_call_target="tpu_custom_call" | custom-call | tf_op jit(solution)/shard_map/pallas_call | solution.py:430
  38.0 1.5 %copy.14 = bf16[16,2048]{1,0:T(8,128)(2,1)} copy(bf16[16,2048]{1,0:T(8,128)(2,1)} %shard_map.118) | data formatting | bytes 131072
where the time goes:
time: 40.1 us; the launch traced here: 39.4 us
  Pallas kernels  38 us (95%)
  local copies, waits for them, and re-layouts  1.47 us (4%)
    pallas_call x1, Pallas kernels, on_device(): pl.pallas_call(functools.partial(layer_kernel, dp, mp), out_shape=jax.Sha...  38 us
    unnamed x1, local copies, waits for them, and re-layouts  1.47 us

commit v1 on v0

v1 whole, which is shorter than its diff:
```python
import contextlib
import functools
import math

import jax
import jax.numpy as jnp
from jax import lax
from jax.experimental import pallas as pl
from jax.experimental.pallas import tpu as pltpu
from jax.sharding import PartitionSpec as P

KEY_VALUE_HEADS = 8
HEAD_SIZE = 128
QUERY_HEADS = 64
GROUP = QUERY_HEADS // KEY_VALUE_HEADS
META = 128
FIRST = 16
SUBS = 2
SIDE = 2
SCOPES = False
MESH = pl.DeviceIdType.MESH

masked_score = -1e30
f32 = jnp.float32
bf16 = jnp.bfloat16


def phase(name):
    return jax.named_scope(name) if SCOPES else contextlib.nullcontext()


def iota(shape, dim):
    return lax.broadcasted_iota(jnp.int32, shape, dim)


def to_column(row):
    n = row.shape[1]
    eye = iota((n, n), 0) == iota((n, n), 1)
    return jnp.sum(jnp.where(eye, row, 0.0), axis=1, keepdims=True)


def to_row(column):
    n = column.shape[0]
    eye = iota((n, n), 0) == iota((n, n), 1)
    return jnp.sum(jnp.where(eye, column, 0.0), axis=0, keepdims=True)


def factors(dp):
    inner = 2 ** (int(math.log2(dp)) // 2)
    return dp // inner, inner


def dot(a, b):
    return jnp.dot(a, b, preferred_element_type=f32)


def pick(table, index):
    value = table[0]
    for i in range(1, len(table)):
        value = jnp.where(index == i, table[i], value)
    return value


def far_first(count):
    return [sorted(range(count), key=lambda t: -abs(t - z)) for z in range(count)]


def relays(z, source, count):
    beyond = z + (1 if z > source else -1)
    return abs(z - source) >= 2 and 0 <= beyond < count


def arrival_order(count):
    def rank(z):
        return lambda s: abs(z - s) - (1.5 if relays(z, s, count) else 0.0)

    return [sorted((s for s in range(count) if s != z), key=rank(z)) for z in range(count)]


def layer_kernel(
    dp,
    mp,
    query_hbm,
    new_key_hbm,
    new_value_hbm,
    key_scale_hbm,
    value_scale_hbm,
    task_hbm,
    length_hbm,
    slot_hbm,
    owner_hbm,
    key_hbm,
    value_hbm,
    weight_hbm,
    out_ref,
    query_ref,
    new_key_ref,
    new_value_ref,
    key_scale_ref,
    value_scale_ref,
    task_ref,
    length_ref,
    slot_ref,
    owner_ref,
    keys,
    values,
    weight,
    rows_f32,
    in_f32,
    fact_rows,
    send_rows,
    recv_rows,
    pair_query,
    pair_small,
    value_scale,
    slot_length,
    slot_context,
    context,
    selector,
    total,
    give,
    take,
    send_part,
    recv_part,
    input_sem,
    fetch_sem,
    request_send,
    request_recv,
    along_send,
    along_recv,
    relay_send,
    across_send,
    across_recv,
    side_send,
    swap_sem,
    part_send,
    part_recv,
):
    me = lax.axis_index("dp")
    part = lax.axis_index("mp")
    rows, query_width = query_ref.shape
    groups = new_key_ref.shape[1] // HEAD_SIZE
    group_width = GROUP * HEAD_SIZE
    segment = group_width + 2 * HEAD_SIZE
    task_total = key_scale_ref.shape[0]
    slots, positions, _ = keys.shape
    capacity = send_rows.shape[1]
    items = dp * capacity
    columns = 2 * weight.shape[2]
    blocks = dp // mp
    half = slots // 2
    per = half // SUBS
    outer, inner = factors(dp)
    z, y = me // inner, lax.rem(me, inner)

    barrier = pltpu.get_barrier_semaphore()
    for k in range(1, dp):
        pl.semaphore_signal(
            barrier, inc=1, device_id=(lax.rem(me + k, dp), part), device_id_type=MESH
        )
    for k in range(1, mp):
        pl.semaphore_signal(
            barrier, inc=1, device_id=(me, lax.rem(part + k, mp)), device_id_type=MESH
        )

    pairs = [
        (task_hbm, task_ref),
        (owner_hbm, owner_ref),
        (length_hbm, length_ref),
        (slot_hbm, slot_ref),
        (key_scale_hbm, key_scale_ref),
        (query_hbm, query_ref),
        (new_key_hbm, new_key_ref),
        (new_value_hbm, new_value_ref),
        (value_scale_hbm, value_scale_ref),
    ]
    inputs = [pltpu.make_async_copy(a, b, input_sem.at[i]) for i, (a, b) in enumerate(pairs)]
    for copy in inputs:
        copy.start()
    parity = lax.rem(part, 2)
    width = weight.shape[2]
    kept_lanes = pl.ds(pl.multiple_of(parity * width, width), width)
    given_lanes = pl.ds(pl.multiple_of((1 - parity) * width, width), width)
    fetches = [
        pltpu.make_async_copy(key_hbm, keys, fetch_sem.at[0]),
        pltpu.make_async_copy(value_hbm, values, fetch_sem.at[1]),
        pltpu.make_async_copy(weight_hbm.at[:, given_lanes], weight.at[0], fetch_sem.at[2]),
        pltpu.make_async_copy(weight_hbm.at[:, kept_lanes], weight.at[1], fetch_sem.at[3]),
    ]
    pair_query[...] = jnp.zeros_like(pair_query)

    def start_of(g):
        return g * segment + (META if g > 0 else 0)

    def span_of(g):
        return slice(start_of(g), start_of(g) + segment + (META if g == 0 else 0))

    meta = slice(segment, segment + META)

    with phase("inputs"):
        for copy in inputs[:4]:
            copy.wait()
    with phase("pack0"):
        task_column = to_column(task_ref[...].astype(f32))
        length_column = to_column(length_ref[...].astype(f32))
        slot_column = to_column(slot_ref[...].astype(f32))
        picked = task_column == iota((rows, task_total), 1).astype(f32)
        owner_column = jnp.sum(
            jnp.where(picked, owner_ref[...].astype(f32), 0.0), axis=1, keepdims=True
        )
        owner_row = to_row(owner_column)
        earlier = iota((rows, rows), 1) < iota((rows, rows), 0)
        rank = jnp.sum(
            jnp.where(earlier & (owner_column == owner_row), 1.0, 0.0), axis=1, keepdims=True
        )
        position_row = to_row(owner_column * capacity + rank)
        packer = jnp.where(
            position_row == iota((items, rows), 0).astype(f32), 1.0, 0.0
        ).astype(bf16)
        side = jnp.floor(slot_column * (1.0 / half))
        pair = slot_column - side * half
        sub = jnp.floor(pair * (1.0 / per))
        line_column = sub * (2 * per) + side * per + (pair - sub * per)
        lane = iota((rows, META), 1)
        line = iota((rows, META), 0)
        task_high = jnp.floor(task_column * (1.0 / 128.0))
        task_low = task_column - task_high * 128.0
        facts = (
            jnp.where(lane == 0, slot_column + 1.0, 0.0)
            + jnp.where(lane == 1, length_column, 0.0)
            + jnp.where(lane == 2, task_high, 0.0)
            + jnp.where(lane == 3, task_low, 0.0)
        )
        shared = jnp.sum(
            jnp.where(lane == FIRST + line, owner_column, 0.0)
            + jnp.where(lane == FIRST + rows + line, line_column, 0.0),
            axis=0,
            keepdims=True,
        )
        rows_f32[:, meta] = dot(packer, facts.astype(bf16)) + shared
        for copy in inputs[4:]:
            copy.wait()
        for fetch in fetches:
            fetch.start()
        key_factor = dot(jnp.where(picked, 1.0, 0.0).astype(bf16), key_scale_ref[...])

    def pack(g):
        own = slice(g * HEAD_SIZE, (g + 1) * HEAD_SIZE)
        at = start_of(g)
        for h in range(GROUP):
            lanes = slice((g * GROUP + h) * HEAD_SIZE, (g * GROUP + h + 1) * HEAD_SIZE)
            scaled = (query_ref[:, lanes].astype(f32) * key_factor[:, own]).astype(bf16)
            rows_f32[:, at + h * HEAD_SIZE : at + (h + 1) * HEAD_SIZE] = dot(packer, scaled)
        first = key_at(g)
        rows_f32[:, first : first + HEAD_SIZE] = dot(packer, new_key_ref[:, own])
        rows_f32[:, first + HEAD_SIZE : first + 2 * HEAD_SIZE] = dot(packer, new_value_ref[:, own])
        for d in range(dp):
            send_rows[d, :, span_of(g)] = rows_f32[
                d * capacity : (d + 1) * capacity, span_of(g)
            ].astype(bf16)

    def key_at(g):
        return start_of(g) + group_width

    far = far_first(outer)
    sends = [(i, j) for i in range(outer) for j in range(inner - 1, -1, -1)][:-1]

    def request_copy(g, i, j):
        target = pick([far[t][i] for t in range(outer)], z) * inner + lax.rem(y + j, inner)
        return pltpu.make_async_remote_copy(
            src_ref=send_rows.at[target, :, span_of(g)],
            dst_ref=recv_rows.at[me, :, span_of(g)],
            send_sem=request_send.at[g, i * inner + j],
            recv_sem=request_recv.at[g, me],
            device_id=(target, part),
            device_id_type=MESH,
        )

    def request_arrival(g, k):
        source = lax.rem(me + k, dp)
        return pltpu.make_async_remote_copy(
            src_ref=send_rows.at[0, :, span_of(g)],
            dst_ref=recv_rows.at[source, :, span_of(g)],
            send_sem=request_send.at[g, 0],
            recv_sem=request_recv.at[g, source],
            device_id=(source, part),
            device_id_type=MESH,
        )

    with phase("pack1"):
        pack(0)
    with phase("barrier"):
        pl.semaphore_wait(barrier, dp + mp - 2)
    for g in range(groups):
        if g > 0:
            with phase("pack2"):
                pack(g)
        for i, j in sends:
            request_copy(g, i, j).start()
    recv_rows[me] = send_rows[me]

    inv_root = 1.0 / math.sqrt(HEAD_SIZE)
    key_line = iota((2 * GROUP, positions), 1).astype(f32)
    low_line = iota((2 * GROUP, positions), 0) < GROUP

    def attend(g, sub):
        own = slice(g * HEAD_SIZE, (g + 1) * HEAD_SIZE)
        picks = [sub * per + i for i in range(per)]

        def both(ref, p):
            return jnp.concatenate([ref[p, :, own], ref[p + half, :, own]], axis=1)

        scores, owns, weights, own_weights, tops, shows, sees = [], [], [], [], [], [], []
        for p in picks:
            scores.append(
                lax.dot_general(
                    pair_query[p].astype(bf16),
                    both(keys, p),
                    (((1,), (1,)), ((), ())),
                    preferred_element_type=f32,
                )
                * inv_root
            )
        for p in picks:
            owns.append(
                jnp.sum(pair_query[p] * pair_small[0, p : p + 1, :], axis=1, keepdims=True)
                * inv_root
            )
        for i, p in enumerate(picks):
            length = jnp.where(
                low_line, slot_length[p : p + 1, :], slot_length[p + half : p + half + 1, :]
            )
            sees.append(key_line < length)
            shows.append(jnp.where(sees[i], scores[i], masked_score))
            tops.append(jnp.maximum(jnp.max(shows[i], axis=1, keepdims=True), owns[i]))
        for i in range(per):
            weights.append(jnp.where(sees[i], jnp.exp(shows[i] - tops[i]), 0.0))
            own_weights.append(jnp.exp(owns[i] - tops[i]))
        blends = [dot(weights[i].astype(bf16), both(values, p)) for i, p in enumerate(picks)]
        for i, p in enumerate(picks):
            weight_sum = jnp.sum(weights[i], axis=1, keepdims=True) + own_weights[i]
            one = slice(p, p + 1)
            blended = blends[i] + own_weights[i].astype(bf16).astype(f32) * pair_small[1, one, :]
            attended = (blended / weight_sum).astype(bf16).astype(f32) * pair_small[2, one, :]
            slot_context[i, :GROUP, :] = attended[:GROUP, :HEAD_SIZE]
            slot_context[i, GROUP:, :] = attended[GROUP:, HEAD_SIZE:]
        for h in range(GROUP):
            context[g, me, sub, :, h * HEAD_SIZE : (h + 1) * HEAD_SIZE] = jnp.concatenate(
                [slot_context[:, h, :], slot_context[:, GROUP + h, :]], axis=0
            ).astype(bf16)

    def near_copy(g, sub, target):
        return pltpu.make_async_remote_copy(
            src_ref=context.at[g, me, sub],
            dst_ref=context.at[g, me, sub],
            send_sem=along_send.at[target, g, sub],
            recv_sem=along_recv.at[z, g, sub],
            device_id=(target * inner + y, part),
            device_id_type=MESH,
        )

    def is_near(target):
        return (target != z) & (target - z < 3) & (z - target < 3)

    def along_arrival(g, sub, source):
        at = source * inner + y
        return pltpu.make_async_remote_copy(
            src_ref=context.at[g, at, sub],
            dst_ref=context.at[g, at, sub],
            send_sem=along_send.at[0, g, sub],
            recv_sem=along_recv.at[source, g, sub],
            device_id=(at, part),
            device_id_type=MESH,
        )

    def relay_copy(g, sub, source):
        at = source * inner + y
        beyond = z + jnp.where(z > source, 1, -1)
        return pltpu.make_async_remote_copy(
            src_ref=context.at[g, at, sub],
            dst_ref=context.at[g, at, sub],
            send_sem=relay_send.at[source, g, sub],
            recv_sem=along_recv.at[source, g, sub],
            device_id=(beyond * inner + y, part),
            device_id_type=MESH,
        )

    def is_relay(source):
        up = (z - source >= 2) & (z < outer - 1)
        down = (source - z >= 2) & (z > 0)
        return up | down

    def across_copy(g, sub, source, j):
        at = source * inner + y
        return pltpu.make_async_remote_copy(
            src_ref=context.at[g, at, sub],
            dst_ref=context.at[g, at, sub],
            send_sem=across_send.at[source, j, g, sub],
            recv_sem=across_recv.at[at, g, sub],
            device_id=(z * inner + lax.rem(y + j, inner), part),
            device_id_type=MESH,
        )

    def across_arrival(g, sub, source, j):
        at = source * inner + lax.rem(y + j, inner)
        return pltpu.make_async_remote_copy(
            src_ref=context.at[g, at, sub],
            dst_ref=context.at[g, at, sub],
            send_sem=across_send.at[0, 0, g, sub],
            recv_sem=across_recv.at[at, g, sub],
            device_id=(at, part),
            device_id_type=MESH,
        )

    chunks = [(g, sub) for g in range(groups) for sub in range(SUBS)]
    side_chunks = SIDE * len(chunks) // 4
    for g in range(groups):
        with phase("requests"):
            for k in range(1, dp):
                request_arrival(g, k).wait_recv()
        with phase("place"):
            for s in range(dp):
                in_f32[s * capacity : (s + 1) * capacity, span_of(g)] = recv_rows[
                    s, :, span_of(g)
                ].astype(f32)
            if g == 0:
                facts_in = in_f32[:, meta]
                for s in range(dp):
                    fact_rows[s] = in_f32[s * capacity : s * capacity + 1, meta]
                placing_row = to_row(facts_in[:, 0:1])
                placer = jnp.where(
                    placing_row == iota((slots, items), 0).astype(f32) + 1.0, 1.0, 0.0
                ).astype(bf16)
                slot_facts = dot(placer, facts_in.astype(bf16))
                slot_task = slot_facts[:, 2:3] * 128.0 + slot_facts[:, 3:4]
                value_scale[...] = dot(
                    jnp.where(slot_task == iota((slots, task_total), 1).astype(f32), 1.0, 0.0).astype(bf16),
                    value_scale_ref[...],
                )
                slot_length[...] = jnp.broadcast_to(slot_facts[:, 1:2], (slots, positions))
            at = start_of(g)
            for h in range(GROUP):
                placed = dot(
                    placer, in_f32[:, at + h * HEAD_SIZE : at + (h + 1) * HEAD_SIZE].astype(bf16)
                )
                pair_query[:, h, :HEAD_SIZE] = placed[:half]
                pair_query[:, GROUP + h, HEAD_SIZE:] = placed[half:]
            for i in range(2):
                first = key_at(g) + i * HEAD_SIZE
                small = dot(placer, in_f32[:, first : first + HEAD_SIZE].astype(bf16))
                pair_small[i, :, :HEAD_SIZE] = small[:half]
                pair_small[i, :, HEAD_SIZE:] = small[half:]
            own = slice(g * HEAD_SIZE, (g + 1) * HEAD_SIZE)
            pair_small[2, :, :HEAD_SIZE] = value_scale[:half, own]
            pair_small[2, :, HEAD_SIZE:] = value_scale[half:, own]
        if g == 0:
            with phase("fetch"):
                fetches[0].wait()
                fetches[1].wait()
        for sub in range(SUBS):
            with phase("attend"):
                attend(g, sub)
            for j in range(1, inner):
                across_copy(g, sub, z, j).start()
            for i in range(outer - 1):
                target = pick([far[t][i] for t in range(outer)], z)

                @pl.when(is_near(target))
                def _():
                    near_copy(g, sub, target).start()

    with phase("selector"):
        lane_r = iota((rows, META), 1)
        line_r = iota((rows, META), 0)
        for i in range(dp):
            fact_row = fact_rows[i]
            owner_in = jnp.sum(
                jnp.where(lane_r == FIRST + line_r, fact_row, 0.0), axis=1, keepdims=True
            )
            line_in = jnp.sum(
                jnp.where(lane_r == FIRST + rows + line_r, fact_row, 0.0), axis=1, keepdims=True
            )
            selector[i * rows : (i + 1) * rows, :] = jnp.where(
                owner_in * slots + line_in == iota((rows, dp * slots), 1).astype(f32), 1.0, 0.0
            ).astype(bf16)

    beside = z + 1 - 2 * lax.rem(z, 2)

    def side_copy(g, sub, j):
        at = z * inner + lax.rem(y + j, inner)
        return pltpu.make_async_remote_copy(
            src_ref=context.at[g, at, sub],
            dst_ref=context.at[g, at, sub],
            send_sem=side_send.at[j, g, sub],
            recv_sem=across_recv.at[at, g, sub],
            device_id=(beside * inner + y, part),
            device_id_type=MESH,
        )

    order = arrival_order(outer)
    late = outer - 2
    events = sorted(
        [(c + (1.5 if r >= late else 0.0), r, c) for c in range(len(chunks)) for r in range(outer - 1)]
        + [(c - 0.5, -1, c) for c in range(side_chunks)]
    )
    with phase("forward"):
        for _, r, c in events:
            g, sub = chunks[c]
            if r < 0:
                for j in range(1, inner):
                    across_arrival(g, sub, z, j).wait_recv()
                    side_copy(g, sub, j).start()
                continue
            source = pick([order[t][r] for t in range(outer)], z)
            along_arrival(g, sub, source).wait_recv()

            @pl.when(is_relay(source))
            def _():
                relay_copy(g, sub, source).start()

            if c < side_chunks:

                @pl.when(source != beside)
                def _():
                    for j in range(1, inner):
                        across_copy(g, sub, source, j).start()

            else:
                for j in range(1, inner):
                    across_copy(g, sub, source, j).start()

    fetches[2].wait()
    fetches[3].wait()

    def arrange(g):
        blocks_of = context[g].reshape(dp * slots, group_width)
        return dot(selector[...], blocks_of).astype(bf16)

    def product(arranged, g, n):
        found = dot(arranged, weight[n, g * group_width : (g + 1) * group_width, :])
        return found.reshape(dp, rows, width)

    def gathered(g):
        for sub in range(SUBS):
            for i in range(outer):
                if i == outer - 1 and chunks.index((g, sub)) < side_chunks:
                    continue
                source = pick([order[t][i] if i < outer - 1 else t for t in range(outer)], z)
                for j in range(1, inner):
                    across_arrival(g, sub, source, j).wait_recv()

    for g in range(groups - 1):
        with phase("across"):
            gathered(g)
        with phase("product"):
            arranged = arrange(g)
            for n in range(2):
                found = product(arranged, g, n)
                total[n] = found if g == 0 else total[n] + found
    with phase("across"):
        gathered(groups - 1)

    partner = part + 1 - 2 * parity
    swap = pltpu.make_async_remote_copy(
        src_ref=give,
        dst_ref=take,
        send_sem=swap_sem.at[0],
        recv_sem=swap_sem.at[1],
        device_id=(me, partner),
        device_id_type=MESH,
    )
    with phase("product"):
        arranged = arrange(groups - 1)
        given = product(arranged, groups - 1, 0)
        give[...] = (given if groups == 1 else given + total[0]).astype(bf16)
    swap.start()
    with phase("product"):
        kept = product(arranged, groups - 1, 1)
        total[1] = kept if groups == 1 else kept + total[1]
    with phase("swap"):
        swap.wait_recv()

    target_part = me // blocks
    place = lax.rem(me, blocks) * mp + part

    def part_target(i, j):
        return pick([far[t][i] for t in range(outer)], z) * inner + lax.rem(y + j, inner)

    def part_copy(i, j):
        target = part_target(i, j)
        return pltpu.make_async_remote_copy(
            src_ref=send_part.at[target],
            dst_ref=recv_part.at[place],
            send_sem=part_send.at[target],
            recv_sem=part_recv.at[place],
            device_id=(target, target_part),
            device_id_type=MESH,
        )
    def part_arrival(j):
        return pltpu.make_async_remote_copy(
            src_ref=send_part.at[0],
            dst_ref=recv_part.at[j],
            send_sem=part_send.at[0],
            recv_sem=part_recv.at[j],
            device_id=(me, part),
            device_id_type=MESH,
        )

    with phase("parts"):
        for i, j in sends + [(outer - 1, 0)]:
            target = part_target(i, j)
            send_part[target] = (total[1, target] + take[target].astype(f32)).astype(bf16)
            if (i, j) in sends:
                part_copy(i, j).start()

        @pl.when(target_part != part)
        def _():
            part_copy(outer - 1, 0).start()

        @pl.when(target_part == part)
        def _():
            recv_part[place] = send_part[me]

        for j in range(blocks * mp):
            stays = (part * blocks + j // mp == me) & (part == j % mp)

            @pl.when(jnp.logical_not(stays))
            def _():
                part_arrival(j).wait_recv()

    for e in range(blocks):
        for n in range(2):
            summed = recv_part[e * mp + n].astype(f32)
            for j in range(n + 2, mp, 2):
                summed = summed + recv_part[e * mp + j].astype(f32)
            first = e * columns + n * width
            out_ref[:, first : first + width] = summed.astype(bf16)

    for g in range(groups):
        for i, j in sends:
            request_copy(g, i, j).wait_send()
    for g, sub in chunks:
        for i in range(outer - 1):
            target = pick([far[t][i] for t in range(outer)], z)

            @pl.when(is_near(target))
            def _():
                near_copy(g, sub, target).wait_send()

            source = pick([order[t][i] for t in range(outer)], z)

            @pl.when(is_relay(source))
            def _():
                relay_copy(g, sub, source).wait_send()

        sided = chunks.index((g, sub)) < side_chunks
        for j in range(1, inner):
            if sided:
                side_copy(g, sub, j).wait_send()
            for source in range(outer):
                if not sided:
                    across_copy(g, sub, source, j).wait_send()
                    continue

                @pl.when(beside != source)
                def _():
                    across_copy(g, sub, source, j).wait_send()

    swap.wait_send()
    for i, j in sends:
        part_copy(i, j).wait_send()

    @pl.when(target_part != part)
    def _():
        part_copy(outer - 1, 0).wait_send()


def on_device(
    dp,
    mp,
    queries,
    incoming_key,
    incoming_value,
    key_cache,
    cached_values,
    task_key_scale,
    task_value_scale,
    out_weight,
    task_id,
    cached_length,
    task_owner,
    cache_slot,
):
    rows, query_width = queries.shape
    kv_width = incoming_key.shape[1]
    slots, positions, _ = key_cache.shape
    capacity = 2 * rows // dp
    items = dp * capacity
    columns = out_weight.shape[1]
    row_width = query_width + 2 * kv_width + META
    groups = kv_width // HEAD_SIZE
    group_width = GROUP * HEAD_SIZE
    half = slots // 2
    per = half // SUBS
    outer, inner = factors(dp)
    away = pl.BlockSpec(memory_space=pl.ANY)
    small = [
        queries,
        incoming_key,
        incoming_value,
        task_key_scale,
        task_value_scale,
        task_id.reshape(1, -1),
        cached_length.reshape(1, -1),
        cache_slot.reshape(1, -1),
        task_owner.reshape(1, -1),
    ]
    return pl.pallas_call(
        functools.partial(layer_kernel, dp, mp),
        out_shape=pltpu.VMEM((rows, dp * columns // mp), bf16),
        in_specs=[away] * 12,
        out_specs=pl.BlockSpec(memory_space=pltpu.VMEM),
        scratch_shapes=[pltpu.VMEM(a.shape, a.dtype) for a in small]
        + [
            pltpu.VMEM(key_cache.shape, bf16),
            pltpu.VMEM(cached_values.shape, bf16),
            pltpu.VMEM((2, out_weight.shape[0], columns // 2), bf16),
            pltpu.VMEM((items, row_width), f32),
            pltpu.VMEM((items, row_width), f32),
            pltpu.VMEM((dp, 1, META), f32),
            pltpu.VMEM((dp, capacity, row_width), bf16),
            pltpu.VMEM((dp, capacity, row_width), bf16),
            pltpu.VMEM((half, 2 * GROUP, 2 * HEAD_SIZE), f32),
            pltpu.VMEM((3, half, 2 * HEAD_SIZE), f32),
            pltpu.VMEM((slots, kv_width), f32),
            pltpu.VMEM((slots, positions), f32),
            pltpu.VMEM((per, 2 * GROUP, HEAD_SIZE), f32),
            pltpu.VMEM((groups, dp, SUBS, 2 * per, group_width), bf16),
            pltpu.VMEM((dp * rows, dp * slots), bf16),
            pltpu.VMEM((2, dp, rows, columns // 2), f32),
            pltpu.VMEM((dp, rows, columns // 2), bf16),
            pltpu.VMEM((dp, rows, columns // 2), bf16),
            pltpu.VMEM((dp, rows, columns // 2), bf16),
            pltpu.VMEM((dp, rows, columns // 2), bf16),
            pltpu.SemaphoreType.DMA((len(small),)),
            pltpu.SemaphoreType.DMA((4,)),
            pltpu.SemaphoreType.DMA((groups, dp)),
            pltpu.SemaphoreType.DMA((groups, dp)),
            pltpu.SemaphoreType.DMA((outer, groups, SUBS)),
            pltpu.SemaphoreType.DMA((outer, groups, SUBS)),
            pltpu.SemaphoreType.DMA((outer, groups, SUBS)),
            pltpu.SemaphoreType.DMA((outer, inner, groups, SUBS)),
            pltpu.SemaphoreType.DMA((dp, groups, SUBS)),
            pltpu.SemaphoreType.DMA((inner, groups, SUBS)),
            pltpu.SemaphoreType.DMA((2,)),
            pltpu.SemaphoreType.DMA((dp,)),
            pltpu.SemaphoreType.DMA((dp,)),
        ],
        compiler_params=pltpu.CompilerParams(
            collective_id=0, has_side_effects=True, vmem_limit_bytes=60 * 1024 * 1024
        ),
    )(*small, key_cache, cached_values, out_weight)


def solution(mesh):
    placed = (
        P("dp", "mp"),
        P("dp", "mp"),
        P("dp", "mp"),
        P("dp", None, "mp"),
        P("dp", None, "mp"),
        P(None, "mp"),
        P(None, "mp"),
        P("mp", "dp"),
        P("dp"),
        P("dp"),
        P(),
        P("dp"),
    )
    return jax.shard_map(
        functools.partial(on_device, mesh.shape["dp"], mesh.shape["mp"]),
        mesh=mesh,
        in_specs=placed,
        out_specs=P("dp", "mp"),
        check_vma=False,
    )
```

time: 40.1 us -> 32.8 us (0.82); the launches traced: 39.4 us -> 32.7 us
  Pallas kernels: 38 us -> 32 us
  local copies, waits for them, and re-layouts: 1.47 us -> 0.63 us
    pallas_call x1, Pallas kernels: 38 us -> 32 us  [on_device(): pl.pallas_call(functools.partial(layer_kernel, dp, mp), out_shape=pltpu.V...]
    unnamed x1, local copies, waits for them, and re-layouts: 1.47 us -> 0.63 us
where the time goes in v1:
time: 32.8 us; the launch traced here: 32.7 us
  Pallas kernels  32 us (98%)
  local copies, waits for them, and re-layouts  0.63 us (2%)
    pallas_call x1, Pallas kernels, on_device(): pl.pallas_call(functools.partial(layer_kernel, dp, mp), out_shape=pltpu.V...  32 us

profile of v1, /device:TPU:0, one launch (start us, length us, event | category | flops | bytes accessed | tf_op | source)
XLA Modules:
  0.0 32.7 jit_solution(2125634477918983275)
XLA Ops:
  0.0 32.0 %shard_map.118 = bf16[16,2048]{1,0:T(8,128)(2,1)S(1)} custom-call(bf16[16,2048]{1,0:T(8,128)(2,1)} %query_hbm.1, bf16[16,256]{1,0:T(8,128)(2,1)} %new_key_hbm.1, bf16[16,256]{1,0:T(8,128)(2,1)} %new_value_hbm.1, bf16[256,256]{1,0:T(8,128)(2,1)} %key_scale_hbm.1, bf16[256,256]{1,0:T(8,128)(2,1)} %value_scale_hbm.1, s32[1,16]{1,0:T(1,128)} %bitcast.5, ...), custom_call_target="tpu_custom_call" | custom-call | tf_op jit(solution)/shard_map/pallas_call | solution.py:718
  32.0 0.6 %copy.14 = bf16[16,2048]{1,0:T(8,128)(2,1)} copy(bf16[16,2048]{1,0:T(8,128)(2,1)S(1)} %shard_map.118) | data formatting | bytes 131072

commit v2 on v1

--- a/solution.py
+++ b/solution.py
@@ -122,19 +122,12 @@
     take,
     send_part,
     recv_part,
-    input_sem,
-    fetch_sem,
-    request_send,
+    local_sem,
     request_recv,
-    along_send,
     along_recv,
-    relay_send,
-    across_send,
     across_recv,
-    side_send,
-    swap_sem,
-    part_send,
-    part_recv,
+    side_recv,
+    last_recv,
 ):
     me = lax.axis_index("dp")
     part = lax.axis_index("mp")
@@ -174,7 +167,7 @@
         (new_value_hbm, new_value_ref),
         (value_scale_hbm, value_scale_ref),
     ]
-    inputs = [pltpu.make_async_copy(a, b, input_sem.at[i]) for i, (a, b) in enumerate(pairs)]
+    inputs = [pltpu.make_async_copy(a, b, local_sem.at[i]) for i, (a, b) in enumerate(pairs)]
     for copy in inputs:
         copy.start()
     parity = lax.rem(part, 2)
@@ -182,10 +175,10 @@
     kept_lanes = pl.ds(pl.multiple_of(parity * width, width), width)
     given_lanes = pl.ds(pl.multiple_of((1 - parity) * width, width), width)
     fetches = [
-        pltpu.make_async_copy(key_hbm, keys, fetch_sem.at[0]),
-        pltpu.make_async_copy(value_hbm, values, fetch_sem.at[1]),
-        pltpu.make_async_copy(weight_hbm.at[:, given_lanes], weight.at[0], fetch_sem.at[2]),
-        pltpu.make_async_copy(weight_hbm.at[:, kept_lanes], weight.at[1], fetch_sem.at[3]),
+        pltpu.make_async_copy(key_hbm, keys, local_sem.at[0]),
+        pltpu.make_async_copy(value_hbm, values, local_sem.at[1]),
+        pltpu.make_async_copy(weight_hbm.at[:, given_lanes], weight.at[0], local_sem.at[2]),
+        pltpu.make_async_copy(weight_hbm.at[:, kept_lanes], weight.at[1], local_sem.at[2]),
     ]
     pair_query[...] = jnp.zeros_like(pair_query)
 
@@ -270,22 +263,15 @@
         return pltpu.make_async_remote_copy(
             src_ref=send_rows.at[target, :, span_of(g)],
             dst_ref=recv_rows.at[me, :, span_of(g)],
-            send_sem=request_send.at[g, i * inner + j],
-            recv_sem=request_recv.at[g, me],
+            send_sem=local_sem.at[3],
+            recv_sem=request_recv.at[g],
             device_id=(target, part),
             device_id_type=MESH,
         )
 
-    def request_arrival(g, k):
-        source = lax.rem(me + k, dp)
-        return pltpu.make_async_remote_copy(
-            src_ref=send_rows.at[0, :, span_of(g)],
-            dst_ref=recv_rows.at[source, :, span_of(g)],
-            send_sem=request_send.at[g, 0],
-            recv_sem=request_recv.at[g, source],
-            device_id=(source, part),
-            device_id_type=MESH,
-        )
+    def requests_done(g):
+        slab = recv_rows.at[pl.ds(0, dp - 1), :, span_of(g)]
+        return pltpu.make_async_copy(slab, slab, request_recv.at[g])
 
     with phase("pack1"):
         pack(0)
@@ -353,8 +339,8 @@
         return pltpu.make_async_remote_copy(
             src_ref=context.at[g, me, sub],
             dst_ref=context.at[g, me, sub],
-            send_sem=along_send.at[target, g, sub],
-            recv_sem=along_recv.at[z, g, sub],
+            send_sem=local_sem.at[4],
+            recv_sem=along_recv.at[z - jnp.where(z > target, 1, 0), g, sub],
             device_id=(target * inner + y, part),
             device_id_type=MESH,
         )
@@ -367,8 +353,8 @@
         return pltpu.make_async_remote_copy(
             src_ref=context.at[g, at, sub],
             dst_ref=context.at[g, at, sub],
-            send_sem=along_send.at[0, g, sub],
-            recv_sem=along_recv.at[source, g, sub],
+            send_sem=local_sem.at[4],
+            recv_sem=along_recv.at[source - jnp.where(source > z, 1, 0), g, sub],
             device_id=(at, part),
             device_id_type=MESH,
         )
@@ -379,8 +365,8 @@
         return pltpu.make_async_remote_copy(
             src_ref=context.at[g, at, sub],
             dst_ref=context.at[g, at, sub],
-            send_sem=relay_send.at[source, g, sub],
-            recv_sem=along_recv.at[source, g, sub],
+            send_sem=local_sem.at[4],
+            recv_sem=along_recv.at[source - jnp.where(source > beyond, 1, 0), g, sub],
             device_id=(beyond * inner + y, part),
             device_id_type=MESH,
         )
@@ -395,29 +381,46 @@
         return pltpu.make_async_remote_copy(
             src_ref=context.at[g, at, sub],
             dst_ref=context.at[g, at, sub],
-            send_sem=across_send.at[source, j, g, sub],
-            recv_sem=across_recv.at[at, g, sub],
+            send_sem=local_sem.at[5],
+            recv_sem=across_recv.at[g],
             device_id=(z * inner + lax.rem(y + j, inner), part),
             device_id_type=MESH,
         )
 
-    def across_arrival(g, sub, source, j):
-        at = source * inner + lax.rem(y + j, inner)
+    def side_first(g, sub, j):
+        at = z * inner + lax.rem(y + j, inner)
+        return pltpu.make_async_remote_copy(
+            src_ref=context.at[g, me, sub],
+            dst_ref=context.at[g, me, sub],
+            send_sem=local_sem.at[5],
+            recv_sem=side_recv.at[g, sub, inner - j - 1],
+            device_id=(at, part),
+            device_id_type=MESH,
+        )
+
+    def side_arrival(g, sub, j):
+        at = z * inner + lax.rem(y + j, inner)
         return pltpu.make_async_remote_copy(
             src_ref=context.at[g, at, sub],
             dst_ref=context.at[g, at, sub],
-            send_sem=across_send.at[0, 0, g, sub],
-            recv_sem=across_recv.at[at, g, sub],
+            send_sem=local_sem.at[5],
+            recv_sem=side_recv.at[g, sub, j - 1],
             device_id=(at, part),
             device_id_type=MESH,
         )
 
+    def across_done(g):
+        count = (outer - 1 if is_sided(g) else outer) * (inner - 1)
+        slab = context.at[g, pl.ds(0, count)]
+        return pltpu.make_async_copy(slab, slab, across_recv.at[g])
+
+    def is_sided(g):
+        return g < SIDE * groups // 4
+
     chunks = [(g, sub) for g in range(groups) for sub in range(SUBS)]
-    side_chunks = SIDE * len(chunks) // 4
     for g in range(groups):
         with phase("requests"):
-            for k in range(1, dp):
-                request_arrival(g, k).wait_recv()
+            requests_done(g).wait()
         with phase("place"):
             for s in range(dp):
                 in_f32[s * capacity : (s + 1) * capacity, span_of(g)] = recv_rows[
@@ -461,7 +464,7 @@
             with phase("attend"):
                 attend(g, sub)
             for j in range(1, inner):
-                across_copy(g, sub, z, j).start()
+                (side_first(g, sub, j) if is_sided(g) else across_copy(g, sub, z, j)).start()
             for i in range(outer - 1):
                 target = pick([far[t][i] for t in range(outer)], z)
 
@@ -491,8 +494,8 @@
         return pltpu.make_async_remote_copy(
             src_ref=context.at[g, at, sub],
             dst_ref=context.at[g, at, sub],
-            send_sem=side_send.at[j, g, sub],
-            recv_sem=across_recv.at[at, g, sub],
+            send_sem=local_sem.at[5],
+            recv_sem=across_recv.at[g],
             device_id=(beside * inner + y, part),
             device_id_type=MESH,
         )
@@ -501,14 +504,14 @@
     late = outer - 2
     events = sorted(
         [(c + (1.5 if r >= late else 0.0), r, c) for c in range(len(chunks)) for r in range(outer - 1)]
-        + [(c - 0.5, -1, c) for c in range(side_chunks)]
+        + [(c - 0.5, -1, c) for c, (g, _) in enumerate(chunks) if is_sided(g)]
     )
     with phase("forward"):
         for _, r, c in events:
             g, sub = chunks[c]
             if r < 0:
                 for j in range(1, inner):
-                    across_arrival(g, sub, z, j).wait_recv()
+                    side_arrival(g, sub, j).wait_recv()
                     side_copy(g, sub, j).start()
                 continue
             source = pick([order[t][r] for t in range(outer)], z)
@@ -518,7 +521,7 @@
             def _():
                 relay_copy(g, sub, source).start()
 
-            if c < side_chunks:
+            if is_sided(g):
 
                 @pl.when(source != beside)
                 def _():
@@ -529,8 +532,7 @@
                 for j in range(1, inner):
                     across_copy(g, sub, source, j).start()
 
-    fetches[2].wait()
-    fetches[3].wait()
+    pltpu.make_async_copy(weight, weight, local_sem.at[2]).wait()
 
     def arrange(g):
         blocks_of = context[g].reshape(dp * slots, group_width)
@@ -540,32 +542,23 @@
         found = dot(arranged, weight[n, g * group_width : (g + 1) * group_width, :])
         return found.reshape(dp, rows, width)
 
-    def gathered(g):
-        for sub in range(SUBS):
-            for i in range(outer):
-                if i == outer - 1 and chunks.index((g, sub)) < side_chunks:
-                    continue
-                source = pick([order[t][i] if i < outer - 1 else t for t in range(outer)], z)
-                for j in range(1, inner):
-                    across_arrival(g, sub, source, j).wait_recv()
-
     for g in range(groups - 1):
         with phase("across"):
-            gathered(g)
+            across_done(g).wait()
         with phase("product"):
             arranged = arrange(g)
             for n in range(2):
                 found = product(arranged, g, n)
                 total[n] = found if g == 0 else total[n] + found
     with phase("across"):
-        gathered(groups - 1)
+        across_done(groups - 1).wait()
 
     partner = part + 1 - 2 * parity
     swap = pltpu.make_async_remote_copy(
         src_ref=give,
         dst_ref=take,
-        send_sem=swap_sem.at[0],
-        recv_sem=swap_sem.at[1],
+        send_sem=local_sem.at[6],
+        recv_sem=last_recv.at[0],
         device_id=(me, partner),
         device_id_type=MESH,
     )
@@ -591,20 +584,14 @@
         return pltpu.make_async_remote_copy(
             src_ref=send_part.at[target],
             dst_ref=recv_part.at[place],
-            send_sem=part_send.at[target],
-            recv_sem=part_recv.at[place],
+            send_sem=local_sem.at[7],
+            recv_sem=last_recv.at[1],
             device_id=(target, target_part),
             device_id_type=MESH,
         )
-    def part_arrival(j):
-        return pltpu.make_async_remote_copy(
-            src_ref=send_part.at[0],
-            dst_ref=recv_part.at[j],
-            send_sem=part_send.at[0],
-            recv_sem=part_recv.at[j],
-            device_id=(me, part),
-            device_id_type=MESH,
-        )
+    def parts_wait(buffer, count, semaphore):
+        slab = buffer.at[pl.ds(0, count)]
+        pltpu.make_async_copy(slab, slab, semaphore).wait()
 
     with phase("parts"):
         for i, j in sends + [(outer - 1, 0)]:
@@ -621,58 +608,46 @@
         def _():
             recv_part[place] = send_part[me]
 
-        for j in range(blocks * mp):
-            stays = (part * blocks + j // mp == me) & (part == j % mp)
-
-            @pl.when(jnp.logical_not(stays))
+        @pl.when(target_part != part)
+        def _():
+            parts_wait(recv_part, dp, last_recv.at[1])
+
+        @pl.when(target_part == part)
+        def _():
+            parts_wait(recv_part, dp - 1, last_recv.at[1])
+
+    with phase("sum"):
+        for e in range(blocks):
+            for n in range(2):
+                summed = recv_part[e * mp + n].astype(f32)
+                for j in range(n + 2, mp, 2):
+                    summed = summed + recv_part[e * mp + j].astype(f32)
+                first = e * columns + n * width
+                out_ref[:, first : first + width] = summed.astype(bf16)
+
+    with phase("drain"):
+        slab = send_rows.at[pl.ds(0, dp - 1)]
+        pltpu.make_async_copy(slab, slab, local_sem.at[3]).wait()
+        for t in range(outer):
+            near = min(2, t) + min(2, outer - 1 - t)
+            relayed = sum(relays(t, s, outer) for s in range(outer))
+
+            @pl.when(z == t)
             def _():
-                part_arrival(j).wait_recv()
-
-    for e in range(blocks):
-        for n in range(2):
-            summed = recv_part[e * mp + n].astype(f32)
-            for j in range(n + 2, mp, 2):
-                summed = summed + recv_part[e * mp + j].astype(f32)
-            first = e * columns + n * width
-            out_ref[:, first : first + width] = summed.astype(bf16)
-
-    for g in range(groups):
-        for i, j in sends:
-            request_copy(g, i, j).wait_send()
-    for g, sub in chunks:
-        for i in range(outer - 1):
-            target = pick([far[t][i] for t in range(outer)], z)
-
-            @pl.when(is_near(target))
-            def _():
-                near_copy(g, sub, target).wait_send()
-
-            source = pick([order[t][i] for t in range(outer)], z)
-
-            @pl.when(is_relay(source))
-            def _():
-                relay_copy(g, sub, source).wait_send()
-
-        sided = chunks.index((g, sub)) < side_chunks
-        for j in range(1, inner):
-            if sided:
-                side_copy(g, sub, j).wait_send()
-            for source in range(outer):
-                if not sided:
-                    across_copy(g, sub, source, j).wait_send()
-                    continue
-
-                @pl.when(beside != source)
-                def _():
-                    across_copy(g, sub, source, j).wait_send()
-
-    swap.wait_send()
-    for i, j in sends:
-        part_copy(i, j).wait_send()
-
-    @pl.when(target_part != part)
-    def _():
-        part_copy(outer - 1, 0).wait_send()
+                slab = context.at[:, pl.ds(0, near + relayed)]
+                pltpu.make_async_copy(slab, slab, local_sem.at[4]).wait()
+
+        slab = context.at[:, pl.ds(0, outer * (inner - 1))]
+        pltpu.make_async_copy(slab, slab, local_sem.at[5]).wait()
+        swap.wait_send()
+
+        @pl.when(target_part != part)
+        def _():
+            parts_wait(send_part, dp, local_sem.at[7])
+
+        @pl.when(target_part == part)
+        def _():
+            parts_wait(send_part, dp - 1, local_sem.at[7])
 
 
 def on_device(
@@ -743,18 +718,11 @@
             pltpu.VMEM((dp, rows, columns // 2), bf16),
             pltpu.VMEM((dp, rows, columns // 2), bf16),
             pltpu.SemaphoreType.DMA((len(small),)),
-            pltpu.SemaphoreType.DMA((4,)),
-            pltpu.SemaphoreType.DMA((groups, dp)),
-            pltpu.SemaphoreType.DMA((groups, dp)),
-            pltpu.SemaphoreType.DMA((outer, groups, SUBS)),
-            pltpu.SemaphoreType.DMA((outer, groups, SUBS)),
-            pltpu.SemaphoreType.DMA((outer, groups, SUBS)),
-            pltpu.SemaphoreType.DMA((outer, inner, groups, SUBS)),
-            pltpu.SemaphoreType.DMA((dp, groups, SUBS)),
-            pltpu.SemaphoreType.DMA((inner, groups, SUBS)),
+            pltpu.SemaphoreType.DMA((groups,)),
+            pltpu.SemaphoreType.DMA((outer - 1, groups, SUBS)),
+            pltpu.SemaphoreType.DMA((groups,)),
+            pltpu.SemaphoreType.DMA((max(groups // 2, 1), SUBS, inner - 1)),
             pltpu.SemaphoreType.DMA((2,)),
-            pltpu.SemaphoreType.DMA((dp,)),
-            pltpu.SemaphoreType.DMA((dp,)),
         ],
         compiler_params=pltpu.CompilerParams(
             collective_id=0, has_side_effects=True, vmem_limit_bytes=60 * 1024 * 1024

time: 32.8 us -> 31.4 us (0.957)
  Pallas kernels: 32 us -> 30.6 us
    pallas_call x1, Pallas kernels: 32 us -> 30.6 us  [on_device(): pl.pallas_call(functools.partial(layer_kernel, dp, mp), out_shape=pltpu.V...]
where the time goes in v2:
time: 31.4 us; the launch traced here: 31.2 us
  Pallas kernels  30.6 us (97%)
  local copies, waits for them, and re-layouts  0.63 us (2%)
    pallas_call x1, Pallas kernels, on_device(): pl.pallas_call(functools.partial(layer_kernel, dp, mp), out_shape=pltpu.V...  30.6 us
    unnamed x1, local copies, waits for them, and re-layouts  0.63 us

profile of v2, /device:TPU:0, one launch (start us, length us, event | category | flops | bytes accessed | tf_op | source)
XLA Modules:
  0.0 31.2 jit_solution(12844681450920379952)
XLA Ops:
  0.0 30.6 %shard_map.118 = bf16[16,2048]{1,0:T(8,128)(2,1)S(1)} custom-call(bf16[16,2048]{1,0:T(8,128)(2,1)} %query_hbm.1, bf16[16,256]{1,0:T(8,128)(2,1)} %new_key_hbm.1, bf16[16,256]{1,0:T(8,128)(2,1)} %new_value_hbm.1, bf16[256,256]{1,0:T(8,128)(2,1)} %key_scale_hbm.1, bf16[256,256]{1,0:T(8,128)(2,1)} %value_scale_hbm.1, s32[1,16]{1,0:T(1,128)} %bitcast.5, ...), custom_call_target="tpu_custom_call" | custom-call | tf_op jit(solution)/shard_map/pallas_call | solution.py:693
  30.6 0.6 %copy.14 = bf16[16,2048]{1,0:T(8,128)(2,1)} copy(bf16[16,2048]{1,0:T(8,128)(2,1)S(1)} %shard_map.118) | data formatting | bytes 131072

commit v3 on v2

--- a/solution.py
+++ b/solution.py
@@ -17,6 +17,9 @@
 FIRST = 16
 SUBS = 2
 SIDE = 2
+END_SIDE = 2.3
+END_LAG = (0.0, 3.5, 3.6)
+MID_LAG = (0.0, 0.1, 0.2)
 SCOPES = False
 MESH = pl.DeviceIdType.MESH
 
@@ -65,9 +68,14 @@
     return [sorted(range(count), key=lambda t: -abs(t - z)) for z in range(count)]
 
 
+def is_near(source, target, count):
+    apart = abs(source - target)
+    return apart == 1 or (apart == 2 and 0 < target < count - 1)
+
+
 def relays(z, source, count):
     beyond = z + (1 if z > source else -1)
-    return abs(z - source) >= 2 and 0 <= beyond < count
+    return z != source and 0 <= beyond < count and not is_near(source, beyond, count)
 
 
 def arrival_order(count):
@@ -345,9 +353,6 @@
             device_id_type=MESH,
         )
 
-    def is_near(target):
-        return (target != z) & (target - z < 3) & (z - target < 3)
-
     def along_arrival(g, sub, source):
         at = source * inner + y
         return pltpu.make_async_remote_copy(
@@ -371,11 +376,6 @@
             device_id_type=MESH,
         )
 
-    def is_relay(source):
-        up = (z - source >= 2) & (z < outer - 1)
-        down = (source - z >= 2) & (z > 0)
-        return up | down
-
     def across_copy(g, sub, source, j):
         at = source * inner + y
         return pltpu.make_async_remote_copy(
@@ -410,13 +410,28 @@
         )
 
     def across_done(g):
-        count = (outer - 1 if is_sided(g) else outer) * (inner - 1)
-        slab = context.at[g, pl.ds(0, count)]
-        return pltpu.make_async_copy(slab, slab, across_recv.at[g])
+        def wait(sources):
+            slab = context.at[g, pl.ds(0, sources * (inner - 1))]
+            pltpu.make_async_copy(slab, slab, across_recv.at[g]).wait()
+
+        if not is_sided(g):
+            wait(outer)
+            return
+
+        @pl.when(at_end)
+        def _():
+            wait(outer - 1)
+
+        @pl.when(jnp.logical_not(at_end))
+        def _():
+            wait(outer)
 
     def is_sided(g):
-        return g < SIDE * groups // 4
-
+        return g >= groups - SIDE * groups // 4
+
+    at_end = (z == 0) | (z == outer - 1)
+    beside = z + 1 - 2 * lax.rem(z, 2)
+    fed = (z == 1) | (z == outer - 2)
     chunks = [(g, sub) for g in range(groups) for sub in range(SUBS)]
     for g in range(groups):
         with phase("requests"):
@@ -464,11 +479,23 @@
             with phase("attend"):
                 attend(g, sub)
             for j in range(1, inner):
-                (side_first(g, sub, j) if is_sided(g) else across_copy(g, sub, z, j)).start()
+                if is_sided(g):
+
+                    @pl.when(at_end)
+                    def _():
+                        side_first(g, sub, j).start()
+
+                    @pl.when(jnp.logical_not(at_end))
+                    def _():
+                        across_copy(g, sub, z, j).start()
+
+                else:
+                    across_copy(g, sub, z, j).start()
             for i in range(outer - 1):
-                target = pick([far[t][i] for t in range(outer)], z)
-
-                @pl.when(is_near(target))
+                targets = [far[t][i] for t in range(outer)]
+                target = pick(targets, z)
+
+                @pl.when(pick([int(is_near(t, o, outer)) for t, o in enumerate(targets)], z) == 1)
                 def _():
                     near_copy(g, sub, target).start()
 
@@ -487,8 +514,6 @@
                 owner_in * slots + line_in == iota((rows, dp * slots), 1).astype(f32), 1.0, 0.0
             ).astype(bf16)
 
-    beside = z + 1 - 2 * lax.rem(z, 2)
-
     def side_copy(g, sub, j):
         at = z * inner + lax.rem(y + j, inner)
         return pltpu.make_async_remote_copy(
@@ -501,12 +526,8 @@
         )
 
     order = arrival_order(outer)
-    late = outer - 2
-    events = sorted(
-        [(c + (1.5 if r >= late else 0.0), r, c) for c in range(len(chunks)) for r in range(outer - 1)]
-        + [(c - 0.5, -1, c) for c, (g, _) in enumerate(chunks) if is_sided(g)]
-    )
-    with phase("forward"):
+
+    def forward(events, end):
         for _, r, c in events:
             g, sub = chunks[c]
             if r < 0:
@@ -514,16 +535,17 @@
                     side_arrival(g, sub, j).wait_recv()
                     side_copy(g, sub, j).start()
                 continue
-            source = pick([order[t][r] for t in range(outer)], z)
+            sources = [order[t][r] for t in range(outer)]
+            source = pick(sources, z)
             along_arrival(g, sub, source).wait_recv()
 
-            @pl.when(is_relay(source))
+            @pl.when(pick([int(relays(t, o, outer)) for t, o in enumerate(sources)], z) == 1)
             def _():
                 relay_copy(g, sub, source).start()
 
-            if is_sided(g):
-
-                @pl.when(source != beside)
+            if is_sided(g) and not end:
+
+                @pl.when(jnp.logical_not(fed & (source == beside)))
                 def _():
                     for j in range(1, inner):
                         across_copy(g, sub, source, j).start()
@@ -532,6 +554,23 @@
                 for j in range(1, inner):
                     across_copy(g, sub, source, j).start()
 
+    def schedule(lags, side_lag):
+        lag = [lags[min(r, len(lags) - 1)] for r in range(outer - 1)]
+        side = [
+            (c + side_lag, -1, c) for c, (g, _) in enumerate(chunks) if side_lag > 0 and is_sided(g)
+        ]
+        return sorted([(c + lag[r], r, c) for c in range(len(chunks)) for r in range(outer - 1)] + side)
+
+    with phase("forward"):
+
+        @pl.when(at_end)
+        def _():
+            forward(schedule(END_LAG, END_SIDE), True)
+
+        @pl.when(jnp.logical_not(at_end))
+        def _():
+            forward(schedule(MID_LAG, 0.0), False)
+
     pltpu.make_async_copy(weight, weight, local_sem.at[2]).wait()
 
     def arrange(g):
@@ -544,14 +583,14 @@
 
     for g in range(groups - 1):
         with phase("across"):
-            across_done(g).wait()
+            across_done(g)
         with phase("product"):
             arranged = arrange(g)
             for n in range(2):
                 found = product(arranged, g, n)
                 total[n] = found if g == 0 else total[n] + found
     with phase("across"):
-        across_done(groups - 1).wait()
+        across_done(groups - 1)
 
     partner = part + 1 - 2 * parity
     swap = pltpu.make_async_remote_copy(
@@ -629,7 +668,7 @@
         slab = send_rows.at[pl.ds(0, dp - 1)]
         pltpu.make_async_copy(slab, slab, local_sem.at[3]).wait()
         for t in range(outer):
-            near = min(2, t) + min(2, outer - 1 - t)
+            near = sum(is_near(t, s, outer) for s in range(outer) if s != t)
             relayed = sum(relays(t, s, outer) for s in range(outer))
 
             @pl.when(z == t)
@@ -637,8 +676,22 @@
                 slab = context.at[:, pl.ds(0, near + relayed)]
                 pltpu.make_async_copy(slab, slab, local_sem.at[4]).wait()
 
-        slab = context.at[:, pl.ds(0, outer * (inner - 1))]
-        pltpu.make_async_copy(slab, slab, local_sem.at[5]).wait()
+        for g in range(groups):
+
+            def drain(sources):
+                slab = context.at[g, pl.ds(0, sources * (inner - 1))]
+                pltpu.make_async_copy(slab, slab, local_sem.at[5]).wait()
+
+            if not is_sided(g):
+                drain(outer)
+                continue
+
+            for more, role in ((1, at_end), (-1, fed), (0, jnp.logical_not(at_end | fed))):
+
+                @pl.when(role)
+                def _():
+                    drain(outer + more)
+
         swap.wait_send()
 
         @pl.when(target_part != part)
@@ -721,7 +774,7 @@
             pltpu.SemaphoreType.DMA((groups,)),
             pltpu.SemaphoreType.DMA((outer - 1, groups, SUBS)),
             pltpu.SemaphoreType.DMA((groups,)),
-            pltpu.SemaphoreType.DMA((max(groups // 2, 1), SUBS, inner - 1)),
+            pltpu.SemaphoreType.DMA((groups, SUBS, inner - 1)),
             pltpu.SemaphoreType.DMA((2,)),
         ],
         compiler_params=pltpu.CompilerParams(

time: 31.4 us -> 29.7 us (0.946)
  Pallas kernels: 30.6 us -> 28.9 us
    pallas_call x1, Pallas kernels: 30.6 us -> 28.9 us  [on_device(): pl.pallas_call(functools.partial(layer_kernel, dp, mp), out_shape=pltpu.V...]
where the time goes in v3:
time: 29.7 us; the launch traced here: 29.6 us
  Pallas kernels  28.9 us (97%)
  local copies, waits for them, and re-layouts  0.63 us (2%)
    pallas_call x1, Pallas kernels, on_device(): pl.pallas_call(functools.partial(layer_kernel, dp, mp), out_shape=pltpu.V...  28.9 us
    unnamed x1, local copies, waits for them, and re-layouts  0.63 us

profile of v3, /device:TPU:0, one launch (start us, length us, event | category | flops | bytes accessed | tf_op | source)
XLA Modules:
  0.0 29.6 jit_solution(8344929766091275893)
XLA Ops:
  0.0 28.9 %shard_map.118 = bf16[16,2048]{1,0:T(8,128)(2,1)S(1)} custom-call(bf16[16,2048]{1,0:T(8,128)(2,1)} %query_hbm.1, bf16[16,256]{1,0:T(8,128)(2,1)} %new_key_hbm.1, bf16[16,256]{1,0:T(8,128)(2,1)} %new_value_hbm.1, bf16[256,256]{1,0:T(8,128)(2,1)} %key_scale_hbm.1, bf16[256,256]{1,0:T(8,128)(2,1)} %value_scale_hbm.1, s32[1,16]{1,0:T(1,128)} %bitcast.5, ...), custom_call_target="tpu_custom_call" | custom-call | tf_op jit(solution)/shard_map/pallas_call | solution.py:746
  29.0 0.6 %copy.14 = bf16[16,2048]{1,0:T(8,128)(2,1)} copy(bf16[16,2048]{1,0:T(8,128)(2,1)S(1)} %shard_map.118) | data formatting | bytes 131072

commit v4 on v3

--- a/solution.py
+++ b/solution.py
@@ -124,6 +124,7 @@
     slot_length,
     slot_context,
     context,
+    last_context,
     selector,
     total,
     give,
@@ -147,7 +148,7 @@
     slots, positions, _ = keys.shape
     capacity = send_rows.shape[1]
     items = dp * capacity
-    columns = 2 * weight.shape[2]
+    columns = weight.shape[1]
     blocks = dp // mp
     half = slots // 2
     per = half // SUBS
@@ -179,14 +180,11 @@
     for copy in inputs:
         copy.start()
     parity = lax.rem(part, 2)
-    width = weight.shape[2]
-    kept_lanes = pl.ds(pl.multiple_of(parity * width, width), width)
-    given_lanes = pl.ds(pl.multiple_of((1 - parity) * width, width), width)
+    width = columns // 2
     fetches = [
         pltpu.make_async_copy(key_hbm, keys, local_sem.at[0]),
         pltpu.make_async_copy(value_hbm, values, local_sem.at[1]),
-        pltpu.make_async_copy(weight_hbm.at[:, given_lanes], weight.at[0], local_sem.at[2]),
-        pltpu.make_async_copy(weight_hbm.at[:, kept_lanes], weight.at[1], local_sem.at[2]),
+        pltpu.make_async_copy(weight_hbm, weight, local_sem.at[2]),
     ]
     pair_query[...] = jnp.zeros_like(pair_query)
 
@@ -339,14 +337,27 @@
             slot_context[i, :GROUP, :] = attended[:GROUP, :HEAD_SIZE]
             slot_context[i, GROUP:, :] = attended[GROUP:, HEAD_SIZE:]
         for h in range(GROUP):
-            context[g, me, sub, :, h * HEAD_SIZE : (h + 1) * HEAD_SIZE] = jnp.concatenate(
+            found = jnp.concatenate(
                 [slot_context[:, h, :], slot_context[:, GROUP + h, :]], axis=0
             ).astype(bf16)
+            if g < groups - 1:
+                context[g, me, sub, :, h * HEAD_SIZE : (h + 1) * HEAD_SIZE] = found
+            else:
+                piece, at = divmod(h, GROUP // SUBS)
+                last_context[
+                    me,
+                    piece,
+                    sub * 2 * per : (sub + 1) * 2 * per,
+                    at * HEAD_SIZE : (at + 1) * HEAD_SIZE,
+                ] = found
+
+    def chunk_at(g, at, sub):
+        return context.at[g, at, sub] if g < groups - 1 else last_context.at[at, sub]
 
     def near_copy(g, sub, target):
         return pltpu.make_async_remote_copy(
-            src_ref=context.at[g, me, sub],
-            dst_ref=context.at[g, me, sub],
+            src_ref=chunk_at(g, me, sub),
+            dst_ref=chunk_at(g, me, sub),
             send_sem=local_sem.at[4],
             recv_sem=along_recv.at[z - jnp.where(z > target, 1, 0), g, sub],
             device_id=(target * inner + y, part),
@@ -356,8 +367,8 @@
     def along_arrival(g, sub, source):
         at = source * inner + y
         return pltpu.make_async_remote_copy(
-            src_ref=context.at[g, at, sub],
-            dst_ref=context.at[g, at, sub],
+            src_ref=chunk_at(g, at, sub),
+            dst_ref=chunk_at(g, at, sub),
             send_sem=local_sem.at[4],
             recv_sem=along_recv.at[source - jnp.where(source > z, 1, 0), g, sub],
             device_id=(at, part),
@@ -368,8 +379,8 @@
         at = source * inner + y
         beyond = z + jnp.where(z > source, 1, -1)
         return pltpu.make_async_remote_copy(
-            src_ref=context.at[g, at, sub],
-            dst_ref=context.at[g, at, sub],
+            src_ref=chunk_at(g, at, sub),
+            dst_ref=chunk_at(g, at, sub),
             send_sem=local_sem.at[4],
             recv_sem=along_recv.at[source - jnp.where(source > beyond, 1, 0), g, sub],
             device_id=(beyond * inner + y, part),
@@ -379,10 +390,10 @@
     def across_copy(g, sub, source, j):
         at = source * inner + y
         return pltpu.make_async_remote_copy(
-            src_ref=context.at[g, at, sub],
-            dst_ref=context.at[g, at, sub],
+            src_ref=chunk_at(g, at, sub),
+            dst_ref=chunk_at(g, at, sub),
             send_sem=local_sem.at[5],
-            recv_sem=across_recv.at[g],
+            recv_sem=across_recv.at[across_at(g, sub)],
             device_id=(z * inner + lax.rem(y + j, inner), part),
             device_id_type=MESH,
         )
@@ -390,8 +401,8 @@
     def side_first(g, sub, j):
         at = z * inner + lax.rem(y + j, inner)
         return pltpu.make_async_remote_copy(
-            src_ref=context.at[g, me, sub],
-            dst_ref=context.at[g, me, sub],
+            src_ref=chunk_at(g, me, sub),
+            dst_ref=chunk_at(g, me, sub),
             send_sem=local_sem.at[5],
             recv_sem=side_recv.at[g, sub, inner - j - 1],
             device_id=(at, part),
@@ -401,18 +412,22 @@
     def side_arrival(g, sub, j):
         at = z * inner + lax.rem(y + j, inner)
         return pltpu.make_async_remote_copy(
-            src_ref=context.at[g, at, sub],
-            dst_ref=context.at[g, at, sub],
+            src_ref=chunk_at(g, at, sub),
+            dst_ref=chunk_at(g, at, sub),
             send_sem=local_sem.at[5],
             recv_sem=side_recv.at[g, sub, j - 1],
             device_id=(at, part),
             device_id_type=MESH,
         )
 
-    def across_done(g):
+    def across_at(g, sub):
+        return g + sub if g == groups - 1 else g
+
+    def across_done(g, sub):
         def wait(sources):
-            slab = context.at[g, pl.ds(0, sources * (inner - 1))]
-            pltpu.make_async_copy(slab, slab, across_recv.at[g]).wait()
+            count = pl.ds(0, sources * (inner - 1))
+            slab = context.at[g, count] if g < groups - 1 else last_context.at[count, sub]
+            pltpu.make_async_copy(slab, slab, across_recv.at[across_at(g, sub)]).wait()
 
         if not is_sided(g):
             wait(outer)
@@ -433,6 +448,28 @@
     beside = z + 1 - 2 * lax.rem(z, 2)
     fed = (z == 1) | (z == outer - 2)
     chunks = [(g, sub) for g in range(groups) for sub in range(SUBS)]
+    def send_own(g, sub):
+        for j in range(1, inner):
+            if is_sided(g):
+
+                @pl.when(at_end)
+                def _():
+                    side_first(g, sub, j).start()
+
+                @pl.when(jnp.logical_not(at_end))
+                def _():
+                    across_copy(g, sub, z, j).start()
+
+            else:
+                across_copy(g, sub, z, j).start()
+        for i in range(outer - 1):
+            targets = [far[t][i] for t in range(outer)]
+            target = pick(targets, z)
+
+            @pl.when(pick([int(is_near(t, o, outer)) for t, o in enumerate(targets)], z) == 1)
+            def _():
+                near_copy(g, sub, target).start()
+
     for g in range(groups):
         with phase("requests"):
             requests_done(g).wait()
@@ -478,26 +515,11 @@
         for sub in range(SUBS):
             with phase("attend"):
                 attend(g, sub)
-            for j in range(1, inner):
-                if is_sided(g):
-
-                    @pl.when(at_end)
-                    def _():
-                        side_first(g, sub, j).start()
-
-                    @pl.when(jnp.logical_not(at_end))
-                    def _():
-                        across_copy(g, sub, z, j).start()
-
-                else:
-                    across_copy(g, sub, z, j).start()
-            for i in range(outer - 1):
-                targets = [far[t][i] for t in range(outer)]
-                target = pick(targets, z)
-
-                @pl.when(pick([int(is_near(t, o, outer)) for t, o in enumerate(targets)], z) == 1)
-                def _():
-                    near_copy(g, sub, target).start()
+            if g < groups - 1:
+                send_own(g, sub)
+        if g == groups - 1:
+            for sub in range(SUBS):
+                send_own(g, sub)
 
     with phase("selector"):
         lane_r = iota((rows, META), 1)
@@ -517,10 +539,10 @@
     def side_copy(g, sub, j):
         at = z * inner + lax.rem(y + j, inner)
         return pltpu.make_async_remote_copy(
-            src_ref=context.at[g, at, sub],
-            dst_ref=context.at[g, at, sub],
+            src_ref=chunk_at(g, at, sub),
+            dst_ref=chunk_at(g, at, sub),
             send_sem=local_sem.at[5],
-            recv_sem=across_recv.at[g],
+            recv_sem=across_recv.at[across_at(g, sub)],
             device_id=(beside * inner + y, part),
             device_id_type=MESH,
         )
@@ -571,98 +593,111 @@
         def _():
             forward(schedule(MID_LAG, 0.0), False)
 
-    pltpu.make_async_copy(weight, weight, local_sem.at[2]).wait()
-
-    def arrange(g):
-        blocks_of = context[g].reshape(dp * slots, group_width)
-        return dot(selector[...], blocks_of).astype(bf16)
-
-    def product(arranged, g, n):
-        found = dot(arranged, weight[n, g * group_width : (g + 1) * group_width, :])
-        return found.reshape(dp, rows, width)
+    fetches[2].wait()
+
+    piece_width = group_width // SUBS
+
+    def product(contexts, first):
+        wide = contexts.shape[-1]
+        arranged = dot(selector[...], contexts.reshape(dp * slots, wide)).astype(bf16)
+        return [
+            dot(
+                arranged, weight[first : first + wide, n * width : (n + 1) * width]
+            ).reshape(dp, rows, width)
+            for n in range(2)
+        ]
+
+    def add(found, started):
+        for n in range(2):
+            total[n] = total[n] + found[n] if started else found[n]
 
     for g in range(groups - 1):
         with phase("across"):
-            across_done(g)
+            across_done(g, 0)
         with phase("product"):
-            arranged = arrange(g)
-            for n in range(2):
-                found = product(arranged, g, n)
-                total[n] = found if g == 0 else total[n] + found
+            add(product(context[g], g * group_width), g > 0)
+    last_first = (groups - 1) * group_width
+    for sub in range(SUBS - 1):
+        with phase("across"):
+            across_done(groups - 1, sub)
+        with phase("product"):
+            add(
+                product(last_context[:, sub], last_first + sub * piece_width),
+                groups > 1 or sub > 0,
+            )
     with phase("across"):
-        across_done(groups - 1)
+        across_done(groups - 1, SUBS - 1)
 
     partner = part + 1 - 2 * parity
-    swap = pltpu.make_async_remote_copy(
-        src_ref=give,
-        dst_ref=take,
-        send_sem=local_sem.at[6],
-        recv_sem=last_recv.at[0],
-        device_id=(me, partner),
-        device_id_type=MESH,
-    )
+
+    def swap(n):
+        return pltpu.make_async_remote_copy(
+            src_ref=give.at[n],
+            dst_ref=take.at[n],
+            send_sem=local_sem.at[6],
+            recv_sem=last_recv.at[0],
+            device_id=(me, partner),
+            device_id_type=MESH,
+        )
+
+    middle = dp // 2
+    kept_at = parity * middle
+    given_at = middle - kept_at
     with phase("product"):
-        arranged = arrange(groups - 1)
-        given = product(arranged, groups - 1, 0)
-        give[...] = (given if groups == 1 else given + total[0]).astype(bf16)
-    swap.start()
-    with phase("product"):
-        kept = product(arranged, groups - 1, 1)
-        total[1] = kept if groups == 1 else kept + total[1]
+        found = product(last_context[:, SUBS - 1], last_first + (SUBS - 1) * piece_width)
+        for n in range(2):
+            total[n] = total[n] + found[n]
+            give[n] = total[n, pl.ds(given_at, middle)].astype(bf16)
+            swap(n).start()
     with phase("swap"):
-        swap.wait_recv()
+        pltpu.make_async_copy(take, take, last_recv.at[0]).wait()
 
     target_part = me // blocks
-    place = lax.rem(me, blocks) * mp + part
-
-    def part_target(i, j):
-        return pick([far[t][i] for t in range(outer)], z) * inner + lax.rem(y + j, inner)
-
-    def part_copy(i, j):
-        target = part_target(i, j)
-        return pltpu.make_async_remote_copy(
-            src_ref=send_part.at[target],
+    lanes_of = mp // 2
+    place = lax.rem(me, blocks) * lanes_of + part // 2
+    stays = (target_part == part) & (me // middle == parity)
+
+    def part_copy(at):
+        return pltpu.make_async_remote_copy(
+            src_ref=send_part.at[at],
             dst_ref=recv_part.at[place],
             send_sem=local_sem.at[7],
             recv_sem=last_recv.at[1],
-            device_id=(target, target_part),
-            device_id_type=MESH,
-        )
+            device_id=(kept_at + at, target_part),
+            device_id_type=MESH,
+        )
+
     def parts_wait(buffer, count, semaphore):
         slab = buffer.at[pl.ds(0, count)]
         pltpu.make_async_copy(slab, slab, semaphore).wait()
 
     with phase("parts"):
-        for i, j in sends + [(outer - 1, 0)]:
-            target = part_target(i, j)
-            send_part[target] = (total[1, target] + take[target].astype(f32)).astype(bf16)
-            if (i, j) in sends:
-                part_copy(i, j).start()
-
-        @pl.when(target_part != part)
+        for at in range(middle):
+            for n in range(2):
+                send_part[at, :, n * width : (n + 1) * width] = (
+                    total[n, kept_at + at] + take[n, at].astype(f32)
+                ).astype(bf16)
+            own = stays & (kept_at + at == me)
+
+            @pl.when(jnp.logical_not(own))
+            def _():
+                part_copy(at).start()
+
+        @pl.when(stays)
         def _():
-            part_copy(outer - 1, 0).start()
-
-        @pl.when(target_part == part)
+            recv_part[place] = send_part[me - kept_at]
+            parts_wait(recv_part, blocks * lanes_of - 1, last_recv.at[1])
+
+        @pl.when(jnp.logical_not(stays))
         def _():
-            recv_part[place] = send_part[me]
-
-        @pl.when(target_part != part)
-        def _():
-            parts_wait(recv_part, dp, last_recv.at[1])
-
-        @pl.when(target_part == part)
-        def _():
-            parts_wait(recv_part, dp - 1, last_recv.at[1])
+            parts_wait(recv_part, blocks * lanes_of, last_recv.at[1])
 
     with phase("sum"):
         for e in range(blocks):
-            for n in range(2):
-                summed = recv_part[e * mp + n].astype(f32)
-                for j in range(n + 2, mp, 2):
-                    summed = summed + recv_part[e * mp + j].astype(f32)
-                first = e * columns + n * width
-                out_ref[:, first : first + width] = summed.astype(bf16)
+            summed = recv_part[e * lanes_of].astype(f32)
+            for j in range(1, lanes_of):
+                summed = summed + recv_part[e * lanes_of + j].astype(f32)
+            out_ref[:, e * columns : (e + 1) * columns] = summed.astype(bf16)
 
     with phase("drain"):
         slab = send_rows.at[pl.ds(0, dp - 1)]
@@ -673,13 +708,13 @@
 
             @pl.when(z == t)
             def _():
-                slab = context.at[:, pl.ds(0, near + relayed)]
+                slab = last_context.at[pl.ds(0, (near + relayed) * groups)]
                 pltpu.make_async_copy(slab, slab, local_sem.at[4]).wait()
 
         for g in range(groups):
 
             def drain(sources):
-                slab = context.at[g, pl.ds(0, sources * (inner - 1))]
+                slab = last_context.at[pl.ds(0, sources * (inner - 1))]
                 pltpu.make_async_copy(slab, slab, local_sem.at[5]).wait()
 
             if not is_sided(g):
@@ -692,15 +727,15 @@
                 def _():
                     drain(outer + more)
 
-        swap.wait_send()
-
-        @pl.when(target_part != part)
+        pltpu.make_async_copy(give, give, local_sem.at[6]).wait()
+
+        @pl.when(stays)
         def _():
-            parts_wait(send_part, dp, local_sem.at[7])
-
-        @pl.when(target_part == part)
+            parts_wait(send_part, middle - 1, local_sem.at[7])
+
+        @pl.when(jnp.logical_not(stays))
         def _():
-            parts_wait(send_part, dp - 1, local_sem.at[7])
+            parts_wait(send_part, middle, local_sem.at[7])
 
 
 def on_device(
@@ -752,7 +787,7 @@
         + [
             pltpu.VMEM(key_cache.shape, bf16),
             pltpu.VMEM(cached_values.shape, bf16),
-            pltpu.VMEM((2, out_weight.shape[0], columns // 2), bf16),
+            pltpu.VMEM(out_weight.shape, bf16),
             pltpu.VMEM((items, row_width), f32),
             pltpu.VMEM((items, row_width), f32),
             pltpu.VMEM((dp, 1, META), f32),
@@ -763,17 +798,18 @@
             pltpu.VMEM((slots, kv_width), f32),
             pltpu.VMEM((slots, positions), f32),
             pltpu.VMEM((per, 2 * GROUP, HEAD_SIZE), f32),
-            pltpu.VMEM((groups, dp, SUBS, 2 * per, group_width), bf16),
+            pltpu.VMEM((max(groups - 1, 1), dp, SUBS, 2 * per, group_width), bf16),
+            pltpu.VMEM((dp, SUBS, slots, group_width // SUBS), bf16),
             pltpu.VMEM((dp * rows, dp * slots), bf16),
             pltpu.VMEM((2, dp, rows, columns // 2), f32),
-            pltpu.VMEM((dp, rows, columns // 2), bf16),
-            pltpu.VMEM((dp, rows, columns // 2), bf16),
-            pltpu.VMEM((dp, rows, columns // 2), bf16),
-            pltpu.VMEM((dp, rows, columns // 2), bf16),
+            pltpu.VMEM((2, dp // 2, rows, columns // 2), bf16),
+            pltpu.VMEM((2, dp // 2, rows, columns // 2), bf16),
+            pltpu.VMEM((dp // 2, rows, columns), bf16),
+            pltpu.VMEM((dp // 2, rows, columns), bf16),
             pltpu.SemaphoreType.DMA((len(small),)),
             pltpu.SemaphoreType.DMA((groups,)),
             pltpu.SemaphoreType.DMA((outer - 1, groups, SUBS)),
-            pltpu.SemaphoreType.DMA((groups,)),
+            pltpu.SemaphoreType.DMA((groups - 1 + SUBS,)),
             pltpu.SemaphoreType.DMA((groups, SUBS, inner - 1)),
             pltpu.SemaphoreType.DMA((2,)),
         ],

time: 29.7 us -> 29.3 us (0.987)
  Pallas kernels: 28.9 us -> 28.5 us
    pallas_call x1, Pallas kernels: 28.9 us -> 28.5 us  [on_device(): pl.pallas_call(functools.partial(layer_kernel, dp, mp), out_shape=pltpu.V...]
where the time goes in v4:
time: 29.3 us; the launch traced here: 29.2 us
  Pallas kernels  28.5 us (97%)
  local copies, waits for them, and re-layouts  0.63 us (2%)
    pallas_call x1, Pallas kernels, on_device(): pl.pallas_call(functools.partial(layer_kernel, dp, mp), out_shape=pltpu.V...  28.5 us
    unnamed x1, local copies, waits for them, and re-layouts  0.63 us

profile of v4, /device:TPU:0, one launch (start us, length us, event | category | flops | bytes accessed | tf_op | source)
XLA Modules:
  0.0 29.2 jit_solution(12990667437054809334)
XLA Ops:
  0.0 28.5 %shard_map.118 = bf16[16,2048]{1,0:T(8,128)(2,1)S(1)} custom-call(bf16[16,2048]{1,0:T(8,128)(2,1)} %query_hbm.1, bf16[16,256]{1,0:T(8,128)(2,1)} %new_key_hbm.1, bf16[16,256]{1,0:T(8,128)(2,1)} %new_value_hbm.1, bf16[256,256]{1,0:T(8,128)(2,1)} %key_scale_hbm.1, bf16[256,256]{1,0:T(8,128)(2,1)} %value_scale_hbm.1, s32[1,16]{1,0:T(1,128)} %bitcast.5, ...), custom_call_target="tpu_custom_call" | custom-call | tf_op jit(solution)/shard_map/pallas_call | solution.py:781
  28.5 0.6 %copy.14 = bf16[16,2048]{1,0:T(8,128)(2,1)} copy(bf16[16,2048]{1,0:T(8,128)(2,1)S(1)} %shard_map.118) | data formatting | bytes 131072

commit v5 on v4

--- a/solution.py
+++ b/solution.py
@@ -174,13 +174,13 @@
         (query_hbm, query_ref),
         (new_key_hbm, new_key_ref),
         (new_value_hbm, new_value_ref),
-        (value_scale_hbm, value_scale_ref),
     ]
     inputs = [pltpu.make_async_copy(a, b, local_sem.at[i]) for i, (a, b) in enumerate(pairs)]
     for copy in inputs:
         copy.start()
     parity = lax.rem(part, 2)
     width = columns // 2
+    scale_fetch = pltpu.make_async_copy(value_scale_hbm, value_scale_ref, local_sem.at[6])
     fetches = [
         pltpu.make_async_copy(key_hbm, keys, local_sem.at[0]),
         pltpu.make_async_copy(value_hbm, values, local_sem.at[1]),
@@ -239,6 +239,7 @@
         rows_f32[:, meta] = dot(packer, facts.astype(bf16)) + shared
         for copy in inputs[4:]:
             copy.wait()
+        scale_fetch.start()
         for fetch in fetches:
             fetch.start()
         key_factor = dot(jnp.where(picked, 1.0, 0.0).astype(bf16), key_scale_ref[...])
@@ -404,7 +405,7 @@
             src_ref=chunk_at(g, me, sub),
             dst_ref=chunk_at(g, me, sub),
             send_sem=local_sem.at[5],
-            recv_sem=side_recv.at[g, sub, inner - j - 1],
+            recv_sem=side_recv.at[groups - 1 - g, sub, inner - j - 1],
             device_id=(at, part),
             device_id_type=MESH,
         )
@@ -415,7 +416,7 @@
             src_ref=chunk_at(g, at, sub),
             dst_ref=chunk_at(g, at, sub),
             send_sem=local_sem.at[5],
-            recv_sem=side_recv.at[g, sub, j - 1],
+            recv_sem=side_recv.at[groups - 1 - g, sub, j - 1],
             device_id=(at, part),
             device_id_type=MESH,
         )
@@ -473,6 +474,8 @@
     for g in range(groups):
         with phase("requests"):
             requests_done(g).wait()
+        if g == 0:
+            scale_fetch.wait()
         with phase("place"):
             for s in range(dp):
                 in_f32[s * capacity : (s + 1) * capacity, span_of(g)] = recv_rows[
@@ -806,11 +809,11 @@
             pltpu.VMEM((2, dp // 2, rows, columns // 2), bf16),
             pltpu.VMEM((dp // 2, rows, columns), bf16),
             pltpu.VMEM((dp // 2, rows, columns), bf16),
-            pltpu.SemaphoreType.DMA((len(small),)),
+            pltpu.SemaphoreType.DMA((len(small) - 1,)),
             pltpu.SemaphoreType.DMA((groups,)),
             pltpu.SemaphoreType.DMA((outer - 1, groups, SUBS)),
             pltpu.SemaphoreType.DMA((groups - 1 + SUBS,)),
-            pltpu.SemaphoreType.DMA((groups, SUBS, inner - 1)),
+            pltpu.SemaphoreType.DMA((max(SIDE * groups // 4, 1), SUBS, inner - 1)),
             pltpu.SemaphoreType.DMA((2,)),
         ],
         compiler_params=pltpu.CompilerParams(

time: 29.3 us -> 29.3 us (level)
  no operation moved by 1% of the time
where the time goes in v5:
time: 29.3 us; the launch traced here: 29.2 us
  Pallas kernels  28.5 us (97%)
  local copies, waits for them, and re-layouts  0.63 us (2%)
    pallas_call x1, Pallas kernels, on_device(): pl.pallas_call(functools.partial(layer_kernel, dp, mp), out_shape=pltpu.V...  28.5 us
    unnamed x1, local copies, waits for them, and re-layouts  0.63 us

profile of v5, /device:TPU:0, one launch (start us, length us, event | category | flops | bytes accessed | tf_op | source)
XLA Modules:
  0.0 29.2 jit_solution(5582119799185903074)
XLA Ops:
  0.0 28.5 %shard_map.118 = bf16[16,2048]{1,0:T(8,128)(2,1)S(1)} custom-call(bf16[16,2048]{1,0:T(8,128)(2,1)} %query_hbm.1, bf16[16,256]{1,0:T(8,128)(2,1)} %new_key_hbm.1, bf16[16,256]{1,0:T(8,128)(2,1)} %new_value_hbm.1, bf16[256,256]{1,0:T(8,128)(2,1)} %key_scale_hbm.1, bf16[256,256]{1,0:T(8,128)(2,1)} %value_scale_hbm.1, s32[1,16]{1,0:T(1,128)} %bitcast.5, ...), custom_call_target="tpu_custom_call" | custom-call | tf_op jit(solution)/shard_map/pallas_call | solution.py:784
  28.5 0.6 %copy.14 = bf16[16,2048]{1,0:T(8,128)(2,1)} copy(bf16[16,2048]{1,0:T(8,128)(2,1)S(1)} %shard_map.118) | data formatting | bytes 131072
